TPU v7x, 512 devices: a whole 4x4x16 slice. The times are simulated.
512 devices in a mesh: lat: 32 (over z_lo, y), lon: 16 (over z_hi, x, core).
Axes of the slice: x: 4, y: 4, z: 16 (z_hi: 2, z_lo: 8; z = z_hi * 8 + z_lo), core: 2. Of those that a mesh axis runs over, the one named last changes fastest.
Arguments:
- grid_field: float32 [384, 256, 2048], P(None, 'lat', 'lon'), may hold values from -6 to 6
- disco_dlat: int32 [256, 16], P('lat'), may hold values from -2 to 2
- disco_dlon: int32 [256, 16], P('lat'), may hold values from -2 to 2
- disco_basis: int32 [256, 16], P('lat'), may hold values from 0 to 3
- disco_quad: float32 [256, 16], P('lat'), may hold values from 0.05 to 0.5
- disco_weight: bfloat16 [4, 384, 384], replicated, may hold values from -0.3125 to 0.3125
- norm_gain: float32 [384], replicated, may hold values from 0.1 to 1.9
- spectral_filter: float32 [384, 256], replicated, may hold values from -6 to 6
- mix_weight: bfloat16 [384, 384], replicated, may hold values from -0.3125 to 0.3125
Outputs:
- updated: float32 [384, 256, 2048], P(None, 'lat', 'lon')
All inputs are finite; a program needn't handle non-finite values.
Results may differ from a plain program's by a relative error of at most 0.0044.
Values may be sent and summed in bfloat16 or wider, within the bound.
No kernel may reach another device: no remote copies, remote signals or barrier semaphores. Data moves between devices by JAX's collectives and lax.ppermute only.
A program may use at most 64 MiB of HBM per device.

v0:
```python
import math

import jax
import jax.numpy as jnp
from jax import lax
from jax.sharding import Mesh
from jax.sharding import PartitionSpec as P

M_DEV = 8
HALO = 2
LON = ("lon_0", "lon_1", "lon_2")


def padded_2(cells, sides, width):
    for axis, dim in sides:
        count = lax.axis_size(axis)
        head = lax.slice_in_dim(cells, 0, width, axis=dim)
        tail = lax.slice_in_dim(cells, cells.shape[dim] - width, cells.shape[dim], axis=dim)
        cells = jnp.concatenate(
            [
                lax.ppermute(tail, axis, [(i, (i + 1) % count) for i in range(count)]),
                cells,
                lax.ppermute(head, axis, [((i + 1) % count, i) for i in range(count)]),
            ],
            axis=dim,
        )
    return cells


def items_in_groups(array, axis, split_dim, concat_dim, work, item_dim, out_dim):
    items = jax.tree.leaves(array)[0].shape[item_dim]
    count = 2 if items % 2 == 0 else 1
    finished = []
    for k in range(count):
        group = jax.tree.map(
            lambda a: lax.slice_in_dim(
                a, k * (items // count), (k + 1) * (items // count), axis=item_dim
            ),
            array,
        )
        finished.append(
            work(
                lax.all_to_all(
                    group, axis, split_axis=split_dim, concat_axis=concat_dim, tiled=True
                )
            )
        )
    return jax.tree.map(lambda *parts: jnp.concatenate(parts, axis=out_dim), *finished)


def split_up(array, dim, devices):
    lengths = array.shape
    tiles = array.reshape(*lengths[:dim], devices, lengths[dim] // devices, *lengths[dim + 1 :])
    return jnp.moveaxis(tiles, dim, 0)


def laid_out(tiles, dim):
    tiles = jnp.moveaxis(tiles, 0, dim)
    lengths = tiles.shape
    return tiles.reshape(*lengths[:dim], lengths[dim] * lengths[dim + 1], *lengths[dim + 2 :])


def exchange_in_order(tiles, axes, turns):
    lengths = [lax.axis_size(a) for a in axes]
    tiles = tiles.reshape(*lengths, *tiles.shape[1:])
    for k in turns:
        tiles = lax.all_to_all(tiles, axes[k], split_axis=k, concat_axis=k, tiled=True)
    return tiles.reshape(-1, *tiles.shape[len(axes) :])


def exchange_by_chip(array, groups, turns, split_dim, concat_dim):
    devices = lax.axis_size(groups[0]) * lax.axis_size(groups[1])
    tiles = split_up(array, split_dim, devices)
    return laid_out(exchange_in_order(tiles, groups, turns), concat_dim)


def legendre_table(first_order, local_orders, all_orders, degrees, nlat):
    lat_pos = jnp.arange(nlat, dtype=jnp.float32)
    colatitude = math.pi * (lat_pos + 0.5) / nlat
    cosine = jnp.cos(colatitude)
    sine = jnp.sin(colatitude)
    counters = jnp.arange(1, all_orders, dtype=jnp.float32)
    cumulative = jnp.concatenate(
        [
            jnp.zeros((1,), jnp.float32),
            jnp.cumsum(jnp.log((2.0 * counters - 1.0) / (2.0 * counters))),
        ]
    )
    log_product = lax.dynamic_slice_in_dim(cumulative, first_order, local_orders)
    orders = first_order + jnp.arange(local_orders, dtype=jnp.int32)
    order_real = orders.astype(jnp.float32)[:, None]
    log_seed = (
        0.5 * (jnp.log((2.0 * order_real + 1.0) / (4.0 * math.pi)) + log_product[:, None])
        + order_real * jnp.log(sine)[None, :]
    )
    rescale = jnp.clip(-log_seed, 0.0, 80.0)
    seed_value = jnp.exp(log_seed + rescale)
    undo = jnp.exp(-rescale)

    def advance(state_pair, degree):
        previous, before_last = state_pair
        degree_real = degree.astype(jnp.float32)
        factor_a = jnp.sqrt(
            jnp.maximum(4.0 * degree_real**2 - 1.0, 1.0)
            / jnp.maximum(degree_real**2 - order_real**2, 1.0)
        )
        factor_b = jnp.sqrt(
            jnp.maximum((degree_real - 1.0) ** 2 - order_real**2, 0.0)
            / jnp.maximum(4.0 * (degree_real - 1.0) ** 2 - 1.0, 1.0)
        )
        recurred = factor_a * (cosine[None, :] * previous - factor_b * before_last)
        current = jnp.where(
            degree == orders[:, None],
            seed_value,
            jnp.where(degree > orders[:, None], recurred, 0.0),
        )
        return ((current, previous), current * undo)

    empty = jnp.zeros((local_orders, nlat), jnp.float32)
    final_pair, table = lax.scan(
        advance, (empty, empty), jnp.arange(degrees, dtype=jnp.int32), unroll=8
    )
    return table


def disco_rows(padded, disco_dlat, disco_dlon, disco_basis, disco_quad, disco_weight, width):
    basis_count = disco_weight.shape[0]
    channels = padded.shape[0]
    zero_index = jnp.zeros((), jnp.int32)

    def one_row(inputs):
        row_index, lat_offsets, lon_offsets, basis_row, quad_row = inputs
        sources = row_index + HALO + lat_offsets
        begins = HALO + lon_offsets

        def take(source, begin):
            return lax.dynamic_slice(padded, (zero_index, source, begin), (channels, 1, width))[
                :, 0, :
            ]

        support = jax.vmap(take)(sources, begins)
        selector = (basis_row[:, None] == jnp.arange(basis_count, dtype=jnp.int32)[None, :]).astype(
            jnp.float32
        ) * quad_row[:, None]
        aggregate = jnp.einsum(
            "kb,kcj->bcj", selector, support, precision=lax.Precision.HIGHEST
        ).astype(jnp.bfloat16)
        return lax.dot_general(
            disco_weight,
            aggregate,
            (((0, 1), (0, 1)), ((), ())),
            preferred_element_type=jnp.float32,
        )

    row_count = disco_dlat.shape[0]
    stacked = lax.map(
        one_row,
        (jnp.arange(row_count, dtype=jnp.int32), disco_dlat, disco_dlon, disco_basis, disco_quad),
    )
    return jnp.transpose(stacked, (1, 0, 2))


def per_device(
    grid_field,
    disco_dlat,
    disco_dlon,
    disco_basis,
    disco_quad,
    disco_weight,
    norm_gain,
    spectral_filter,
    mix_weight,
):
    lat_count = lax.axis_size("lat")
    lon_count = lax.axis_size(LON)
    channels, lat_local, lon_local = grid_field.shape
    lat_total = lat_local * lat_count
    lon_total = lon_local * lon_count
    mode_count = M_DEV * lat_count
    chan_local = channels // lon_count
    lat_index = lax.axis_index("lat")
    lon_index = lax.axis_index(LON)
    wrapped = padded_2(grid_field.astype(jnp.bfloat16), (("lat", 1), (LON, 2)), HALO).astype(
        grid_field.dtype
    )
    global_rows = lat_index * lat_local + jnp.arange(lat_local + 2 * HALO, dtype=jnp.int32) - HALO
    inside = (global_rows >= 0) & (global_rows < lat_total)
    padded = jnp.where(inside[None, :, None], wrapped, 0.0)
    after_conv = grid_field + disco_rows(
        padded, disco_dlat, disco_dlon, disco_basis, disco_quad, disco_weight, lon_local
    )
    mean_square = jnp.mean(after_conv * after_conv, axis=0, keepdims=True)
    normed = after_conv * lax.rsqrt(mean_square + 1e-06) * norm_gain[:, None, None]
    lon_pos = jnp.arange(lon_total, dtype=jnp.int32)
    mode_pos = jnp.arange(mode_count, dtype=jnp.int32)
    phase = (lon_pos[:, None] * mode_pos[None, :] % lon_total).astype(jnp.float32) * (
        2.0 * math.pi / lon_total
    )
    cos_part = jnp.cos(phase)
    sin_part = jnp.sin(phase)
    forward_table = jnp.concatenate([cos_part, -sin_part], axis=1) * (2.0 * math.pi / lon_total)
    mode_weight = jnp.where(mode_pos == 0, 1.0, 2.0).astype(jnp.float32)[None, :]
    inverse_table = jnp.transpose(
        jnp.concatenate([cos_part * mode_weight, -sin_part * mode_weight], axis=1)
    )
    portion = lax.all_to_all(
        normed.astype(jnp.bfloat16), LON, split_axis=0, concat_axis=2, tiled=True
    ).astype(normed.dtype)
    result = jnp.einsum("crj,jq->qcr", portion, forward_table, precision=lax.Precision.HIGHEST)
    fourier = result.reshape(2, mode_count, portion.shape[0], portion.shape[1])
    table = legendre_table(lat_index * M_DEV, M_DEV, mode_count, mode_count, lat_total)
    lat_pos = jnp.arange(lat_total, dtype=jnp.float32)
    quad_weight = math.pi / lat_total * jnp.sin(math.pi * (lat_pos + 0.5) / lat_total)
    local_filter = lax.dynamic_slice_in_dim(spectral_filter, lon_index * chan_local, chan_local, 0)

    def legendre_pass(portion):
        weighted = portion * quad_weight
        spectra = jnp.einsum("rmck,lmk->rmcl", weighted, table, precision=lax.Precision.HIGHEST)
        filtered = spectra * local_filter[None, None]
        return jnp.einsum("rmcl,lmk->rmck", filtered, table, precision=lax.Precision.HIGHEST)

    synthesis = items_in_groups(fourier, "lat", 1, 3, legendre_pass, 0, 0)
    returned = lax.all_to_all(synthesis, "lat", split_axis=3, concat_axis=1, tiled=True)
    wave_field = jnp.einsum(
        "qcr,qj->crj",
        returned.reshape(2 * mode_count, chan_local, lat_local),
        inverse_table,
        precision=lax.Precision.HIGHEST,
    )
    activated_local = jax.nn.gelu(wave_field, approximate=True).astype(jnp.bfloat16)
    activated = exchange_by_chip(activated_local, (("lon_0", "lon_1"), "lon_2"), (1, 0), 2, 0)
    mixed = lax.dot_general(
        mix_weight, activated, (((0,), (0,)), ((), ())), preferred_element_type=jnp.float32
    )
    return after_conv + mixed


def solution(mesh):
    torus = Mesh(
        mesh.devices.reshape(mesh.shape["lat"], 2, 4, 2), ("lat", "lon_0", "lon_1", "lon_2")
    )
    placed = (
        P(None, "lat", LON),
        P("lat", None),
        P("lat", None),
        P("lat", None),
        P("lat", None),
        P(),
        P(),
        P(),
        P(),
    )
    return jax.shard_map(
        per_device, mesh=torus, in_specs=placed, out_specs=P(None, "lat", LON), check_vma=False
    )
```

profile of v0, /device:TPU:32, one launch (start us, length us, event | category | flops | bytes accessed | tf_op | source)
XLA Modules:
  0.0 788.3 jit_solution(13659093501245691786)
XLA Ops:
  2.4 3.5 collective-permute-start
  5.9 4.5 collective-permute-start.1
  16.2 15.3 %collective-permute-start.3 = (bf16[384,12,2]{0,1,2:T(8,128)(2,1)S(1)}, bf16[384,12,2]{0,1,2:T(8,128)(2,1)S(1)}, u32[]{:S(2)}, u32[]{:S(2)}) collective-permute-start(bf16[384,12,2]{0,1,2:T(8,128)(2,1)S(1)} %get-tuple-element.569), channel_id=1, source_target_pairs={{1,0},{2,1},{3,2},{4,3},{5,4},{6,5},{7,6},{8,7},{9,8},{10,9},{11,1... | collective-permute-start | bytes 55304 | tf_op jit(solution)/shard_map/ppermute | solution.py:23
  35.9 124.9 %while.33 = (s32[]{:T(128)}, f32[8,384,128]{1,2,0:T(8,128)}, s32[8,16]{1,0:T(8,128)}, f32[8,16]{1,0:T(8,128)}, s32[8]{0:T(128)S(1)}, /*index=5*/s32[8,16]{1,0:T(...) while((s32[]{:T(128)}, f32[8,384,128]{1,2,0:T(8,128)}, ...), condition=%wide.region_1.2_spmd, body=%wide.region_0.1_spmd.sunk | while | flops 188940624 | bytes 22611376 | solution.py:156
  37.9 6.7 gather_fusion
  44.6 2.7 copy.133
  53.4 6.7 gather_fusion
  60.1 2.7 copy.133
  68.9 6.7 gather_fusion
  84.5 7.2 gather_fusion
  100.5 6.8 gather_fusion
  116.2 6.8 gather_fusion
  131.8 6.6 gather_fusion
  147.2 6.7 gather_fusion
  166.3 15.8 %all-to-all-start = ((bf16[384,8,128]{2,1,0:T(8,128)(2,1)}), bf16[384,8,128]{2,1,0:T(8,128)(2,1)S(1)}, u32[]{:S(2)}, u32[]{:S(2)}) async-start(bf16[384,8,128]{2,1,0:T(8,128)(2,1)} %copy.69), calls=%async_computation | async-start | bytes 1572864 | tf_op jit(solution)/shard_map/all_to_all | solution.py:206
  182.7 9.2 %sine_negate_fusion = (f32[2048,256]{1,0:T(8,128)}, f32[2048,256]{1,0:T(8,128)}) fusion(), kind=kLoop, calls=%fused_computation.116 | loop fusion | flops 7864320 | bytes 4194304 | tf_op jit(solution)/shard_map/neg | solution.py:201
  191.9 37.8 %all-to-all-done = bf16[384,8,128]{2,1,0:T(8,128)(2,1)S(1)} async-done(((bf16[384,8,128]{2,1,0:T(8,128)(2,1)}), bf16[384,8,128]{2,1,0:T(8,128)(2,1)S(1)}, u32[]{:S(2)}, u32[]{:S(2)}) %all-to-all-start) | async-done | bytes 786464 | tf_op jit(solution)/shard_map/all_to_all | solution.py:206
  232.6 4.2 fusion.59
  238.2 2.7 reshape.617
  240.9 11.9 %all-to-all-start.1 = ((f32[32,1,1536]{2,1,0:T(1,128)}), f32[32,1,1536]{2,1,0:T(1,128)S(1)}, u32[]{:S(2)}, u32[]{:S(2)}) async-start(f32[32,1,1536]{2,1,0:T(1,128)} %reshape.617), calls=%async_computation.1 | async-start | bytes 393216 | tf_op jit(solution)/shard_map/all_to_all | solution.py:43
  257.1 11.3 %all-to-all-done.1 = f32[32,1,1536]{2,1,0:T(1,128)S(1)} async-done(((f32[32,1,1536]{2,1,0:T(1,128)}), f32[32,1,1536]{2,1,0:T(1,128)S(1)}, u32[]{:S(2)}, u32[]{:S(2)}) %all-to-all-start.1) | async-done | bytes 196640 | tf_op jit(solution)/shard_map/all_to_all | solution.py:43
  268.4 6.6 all-to-all-start.2
  275.0 378.0 %while.34 = (s32[]{:T(128)}, f32[8,256]{1,0:T(8,128)S(1)}, f32[8,256]{1,0:T(8,128)S(1)}, f32[32,8,8,256]{3,2,1,0:T(8,128)S(1)}, s32[32,8]{0,1:T(8,128)S(1)}, /*i...) while((s32[]{:T(128)}, f32[8,256]{1,0:T(8,128)S(1)}, ...), condition=%wide.region_5.6_spmd.clone.clone.clone.clone, body=%wide.region_4.5_spmd.clone.clone.clone.clone.sunk | while | flops 370002 | bytes 440491 | solution.py:120
  657.6 3.3 fusion.110
  667.6 3.3 fusion.104
  674.0 2.7 reshape.619
  676.7 12.6 %all-to-all-start.3 = ((f32[32,1,3072]{2,1,0:T(1,128)}), f32[32,1,3072]{2,1,0:T(1,128)S(1)}, u32[]{:S(2)}, u32[]{:S(2)}) async-start(f32[32,1,3072]{2,1,0:T(1,128)} %reshape.619), calls=%async_computation.3 | async-start | bytes 786432 | tf_op jit(solution)/shard_map/all_to_all | solution.py:223
  689.3 9.4 %broadcast_multiply_fusion.1 = (f32[2048,256]{1,0:T(8,128)}, f32[2048,256]{1,0:T(8,128)}) fusion(f32[256]{0:T(256)S(1)} %compare_select_fusion.2), kind=kLoop, calls=%fused_computation.153 | loop fusion | flops 8912896 | bytes 4195328 | tf_op jit(solution)/shard_map/mul | solution.py:204
  698.7 12.9 %all-to-all-done.3 = f32[32,1,3072]{2,1,0:T(1,128)S(1)} async-done(((f32[32,1,3072]{2,1,0:T(1,128)}), f32[32,1,3072]{2,1,0:T(1,128)S(1)}, u32[]{:S(2)}, u32[]{:S(2)}) %all-to-all-start.3) | async-done | bytes 393248 | tf_op jit(solution)/shard_map/all_to_all | solution.py:223
  719.1 6.1 fusion.88
  725.5 4.5 all_to_all.79
  730.0 54.0 %all_to_all.80 = bf16[8,2,24,8,128]{4,3,2,1,0:T(8,128)(2,1)S(1)} all-to-all(bf16[8,2,24,8,128]{4,3,2,1,0:T(8,128)(2,1)S(1)} %copy.87), channel_id=1, replica_groups=mesh['lat'=32,'lon_0'=2,'lon_1'=4,'lon_2'=2] {'lon_0','lon_1'}, dimensions={0} | all-to-all | bytes 1572864 | tf_op jit(solution)/shard_map/all_to_all | solution.py:67
  (1041 shorter events, 323.9 us)
Async XLA Ops:
  0.0 653.1 %copy-start = (f32[384,256]{1,0:T(8,128)S(1)}, f32[384,256]{1,0:T(8,128)}, u32[]{:S(2)}) copy-start(f32[384,256]{1,0:T(8,128)} %param.20) | copy-start | bytes 1179652
  0.0 31.6 %copy-start.4 = (f32[384,8,128]{2,1,0:T(8,128)S(1)}, f32[384,8,128]{2,1,0:T(8,128)}, u32[]{:S(2)}) copy-start(f32[384,8,128]{2,1,0:T(8,128)} %param.13) | copy-start | bytes 4718596
  2.4 10.6 %collective-permute-start = (bf16[384,2,128]{0,1,2:T(2,128)(2,1)S(1)}, bf16[384,2,128]{0,1,2:T(2,128)(2,1)S(1)}, u32[]{:S(2)}, u32[]{:S(2)}) collective-permute-start(bf16[384,2,128]{0,1,2:T(2,128)(2,1)S(1)} %get-tuple-element.570), channel_id=1, source_target_pairs={{0,16},{16,32},{32,48},{48,64},{64,80},{80,96},{96,112},{112,128},... | collective-permute-start | bytes 589832 | tf_op jit(solution)/shard_map/ppermute | solution.py:21
  5.9 8.3 %collective-permute-start.1 = (bf16[384,2,128]{0,1,2:T(2,128)(2,1)S(1)}, bf16[384,2,128]{0,1,2:T(2,128)(2,1)S(1)}, u32[]{:S(2)}, u32[]{:S(2)}) collective-permute-start(bf16[384,2,128]{0,1,2:T(2,128)(2,1)S(1)} %get-tuple-element.571), channel_id=1, source_target_pairs={{16,0},{32,16},{48,32},{64,48},{80,64},{96,80},{112,96},{128,112},... | collective-permute-start | bytes 589832 | tf_op jit(solution)/shard_map/ppermute | solution.py:23
  14.3 19.0 %collective-permute-start.2 = (bf16[384,12,2]{0,1,2:T(8,128)(2,1)S(1)}, bf16[384,12,2]{0,1,2:T(8,128)(2,1)S(1)}, u32[]{:S(2)}, u32[]{:S(2)}) collective-permute-start(bf16[384,12,2]{0,1,2:T(8,128)(2,1)S(1)} %get-tuple-element.568), channel_id=1, source_target_pairs={{0,1},{1,2},{2,3},{3,4},{4,5},{5,6},{6,7},{7,8},{8,9},{9,10},{10,1... | collective-permute-start | bytes 55304 | tf_op jit(solution)/shard_map/ppermute | solution.py:21
  16.2 17.1 %collective-permute-start.3 = (bf16[384,12,2]{0,1,2:T(8,128)(2,1)S(1)}, bf16[384,12,2]{0,1,2:T(8,128)(2,1)S(1)}, u32[]{:S(2)}, u32[]{:S(2)}) collective-permute-start(bf16[384,12,2]{0,1,2:T(8,128)(2,1)S(1)} %get-tuple-element.569), channel_id=1, source_target_pairs={{1,0},{2,1},{3,2},{4,3},{5,4},{6,5},{7,6},{8,7},{9,8},{10,9},{11,1... | collective-permute-start | bytes 55304 | tf_op jit(solution)/shard_map/ppermute | solution.py:23
  47.2 3.1 copy-start.1
  62.8 3.1 copy-start.1
  78.3 3.1 copy-start.1
  94.4 3.1 copy-start.1
  110.0 3.1 copy-start.1
  125.7 3.1 copy-start.1
  141.1 3.1 copy-start.1
  156.6 3.1 copy-start.1
  160.9 2.4 copy-start.2
  160.9 2.4 copy-start.8
  166.3 63.4 %all-to-all-start = ((bf16[384,8,128]{2,1,0:T(8,128)(2,1)}), bf16[384,8,128]{2,1,0:T(8,128)(2,1)S(1)}, u32[]{:S(2)}, u32[]{:S(2)}) async-start(bf16[384,8,128]{2,1,0:T(8,128)(2,1)} %copy.69), calls=%async_computation | async-start | bytes 1572864 | tf_op jit(solution)/shard_map/all_to_all | solution.py:206
  240.9 27.5 %all-to-all-start.1 = ((f32[32,1,1536]{2,1,0:T(1,128)}), f32[32,1,1536]{2,1,0:T(1,128)S(1)}, u32[]{:S(2)}, u32[]{:S(2)}) async-start(f32[32,1,1536]{2,1,0:T(1,128)} %reshape.617), calls=%async_computation.1 | async-start | bytes 393216 | tf_op jit(solution)/shard_map/all_to_all | solution.py:43
  268.4 394.9 %all-to-all-start.2 = ((f32[32,1,1536]{2,1,0:T(1,128)}), f32[32,1,1536]{2,1,0:T(1,128)}, u32[]{:S(2)}, u32[]{:S(2)}) async-start(f32[32,1,1536]{2,1,0:T(1,128)} %reshape.615), calls=%async_computation.2 | async-start | bytes 393216 | tf_op jit(solution)/shard_map/all_to_all | solution.py:43
  667.6 5.1 copy-start.6
  676.7 34.9 %all-to-all-start.3 = ((f32[32,1,3072]{2,1,0:T(1,128)}), f32[32,1,3072]{2,1,0:T(1,128)S(1)}, u32[]{:S(2)}, u32[]{:S(2)}) async-start(f32[32,1,3072]{2,1,0:T(1,128)} %reshape.619), calls=%async_computation.3 | async-start | bytes 786432 | tf_op jit(solution)/shard_map/all_to_all | solution.py:223
  716.7 2.5 copy-start.5
  725.4 58.6 %copy-start.3 = (f32[384,8,128]{0,2,1:T(8,128)S(1)}, f32[384,8,128]{0,2,1:T(8,128)}, u32[]{:S(2)}) copy-start(f32[384,8,128]{0,2,1:T(8,128)} %copy.68) | copy-start | bytes 4718596
  725.4 58.6 %copy-start.7 = (bf16[384,384]{1,0:T(8,128)(2,1)S(1)}, bf16[384,384]{1,0:T(8,128)(2,1)}, u32[]{:S(2)}) copy-start(bf16[384,384]{1,0:T(8,128)(2,1)} %param.21) | copy-start | bytes 884740
where the time goes:
time: 801 us; the launch traced here: 788 us
  other arithmetic  226 us (28%)
  loops' own time  172 us (21%)
  local copies, waits for them, and re-layouts  147 us (18%)
  starting transfers between devices  72 us (9%)
  waiting for transfers between devices  66 us (8%)
  blocking collectives  58.5 us (7%)
  matrix products  44.8 us (6%)
    another operation x1, loops' own time, legendre_table(): lax.scan(advance, (empty, empty), jnp.arange(degrees, dtype=jnp.int32), u...  167 us
    gt x256, other arithmetic, advance(): degree > orders[:, None]  159 us
    gather x16, local copies, waits for them, and re-layouts, take(): lax.dynamic_slice(padded, (zero_index, source, begin), (channels, 1, width))  75.6 us
    all_to_all x2, blocking collectives, exchange_in_order(): lax.all_to_all(tiles, axes[k], split_axis=k, concat_axis=k, tiled=True)  58.5 us
    all_to_all x1, waiting for transfers between devices, per_device(): lax.all_to_all(normed.astype(jnp.bfloat16), LON, split_axis=0, concat_axi...  37.8 us
    while x224, other arithmetic  20.9 us
    ppermute x2, starting transfers between devices, padded_2(): lax.ppermute(head, axis, [((i + 1) % count, i) for i in range(count)])  19.8 us
    slice x32, local copies, waits for them, and re-layouts, legendre_table(): lax.scan(advance, (empty, empty), jnp.arange(degrees, dtype=jnp.int32), u...  19.4 us
  transfers between devices with their start and end apart: 8, of which 5 were waited for; matrix products, arithmetic and copies ran while one was open for 31% of the time, Pallas kernels for 0%

commit v1 on v0

v1 whole, which is shorter than its diff:
```python
import math

import jax
import jax.numpy as jnp
import numpy as np
from jax import lax
from jax.experimental import pallas as pl
from jax.experimental.pallas import tpu as pltpu
from jax.sharding import Mesh
from jax.sharding import PartitionSpec as P

C = 384
NLAT = 256
NLON = 2048
MM = 256
LL = 256
KSUP = 16
NBASIS = 4
TL = 8
JL = 128
CB = 12
ORD = 16
LAT = ("zl", "y")
LON = ("zh", "x", "core")
CHAN = ("y", "x", "core")
RING = ("zh", "zl")
F32 = jnp.float32
BF16 = jnp.bfloat16


def call(kernel, name, out_shape, in_specs=None, scratch=(), grid=None, out_specs=None):
    kwargs = {}
    if grid is not None:
        kwargs["grid"] = grid
    if in_specs is not None:
        kwargs["in_specs"] = in_specs
    if out_specs is not None:
        kwargs["out_specs"] = out_specs
    return pl.pallas_call(
        kernel,
        out_shape=out_shape,
        scratch_shapes=list(scratch),
        name=name,
        compiler_params=pltpu.CompilerParams(vmem_limit_bytes=60 * 1024 * 1024),
        **kwargs,
    )


def shape(dims, kind=BF16):
    return jax.ShapeDtypeStruct(dims, kind)


def dot(a, b, dims=((1,), (0,))):
    return lax.dot_general(a, b, (dims, ((), ())), preferred_element_type=F32)


def two_parts(value):
    high = value.astype(BF16)
    return high, (value - high.astype(F32)).astype(BF16)


def split_constant(table):
    high = table.astype(np.float32).astype(jnp.bfloat16)
    low = (table - high.astype(np.float64)).astype(np.float32).astype(jnp.bfloat16)
    return high, low


def longitude_tables():
    order = np.arange(MM)
    lon = np.arange(NLON // 2)
    phase = (order[:, None] * lon[None, :] % NLON) * (2.0 * math.pi / NLON)
    cosine, sine = np.cos(phase), -np.sin(phase)
    both = np.stack([cosine, sine]).reshape(2, MM // ORD, ORD, NLON // 2)
    both = both.transpose(1, 0, 2, 3).reshape(2 * MM, NLON // 2)
    weight = np.where(order == 0, 1.0, 2.0).reshape(MM // ORD, 1, ORD)
    weight = np.broadcast_to(weight, (MM // ORD, 2, ORD)).reshape(2 * MM, 1)
    return split_constant(both * (2.0 * math.pi / NLON)), split_constant(both * weight)


def lane_order():
    y, c, t = np.meshgrid(np.arange(4), np.arange(CB), np.arange(TL), indexing="ij")
    src = (y * CB + c) * TL + t
    dst = ((c // 4 * 4 + y) * TL + t) * 4 + c % 4
    out = np.zeros((4 * CB * TL, 4 * CB * TL), np.float32)
    out[src.ravel(), dst.ravel()] = 1.0
    return out.astype(jnp.bfloat16)


def latitude_rows():
    lane = np.arange(NLAT)
    lat = lane % 8 * 32 + lane // 8
    colat = math.pi * (lat + 0.5) / NLAT
    rows = np.zeros((8, NLAT), np.float32)
    rows[0] = np.cos(colat)
    rows[1] = np.log(np.sin(colat))
    rows[2] = math.pi / NLAT * np.sin(colat)
    return rows


def order_terms():
    order = np.arange(MM, dtype=np.float64)
    steps = np.zeros(MM)
    steps[1:] = np.cumsum(np.log((2.0 * order[1:] - 1.0) / (2.0 * order[1:])))
    term = 0.5 * (np.log((2.0 * order + 1.0) / (4.0 * math.pi)) + steps)
    return np.repeat(term[:, None], 128, axis=1).astype(np.float32)


def degree_terms():
    degree = np.arange(LL, dtype=np.float64)
    return np.stack(
        [
            np.sqrt(np.maximum(4.0 * degree**2 - 1.0, 1.0)),
            1.0 / np.sqrt(np.maximum(4.0 * (degree - 1.0) ** 2 - 1.0, 1.0)),
        ]
    ).astype(np.float32)


def rows_kernel(x_ref, first_ref, last_ref):
    for u in range(2):
        first_ref[pl.ds(u * C, C), :] = x_ref[pl.ds(u, C, stride=TL), :].astype(BF16)
        last_ref[pl.ds(u * C, C), :] = x_ref[pl.ds(TL - 2 + u, C, stride=TL), :].astype(BF16)


def edges_kernel(x_ref, up_ref, down_ref, head_ref, tail_ref):
    row = lax.broadcasted_iota(jnp.int32, (64, JL), 0)
    lane = lax.broadcasted_iota(jnp.int32, (64, JL), 1)
    total = jnp.zeros((64, C), F32)
    for r in range(12):
        if r < 2:
            cells = up_ref[pl.ds(r * C, C), :]
        elif r < 10:
            cells = x_ref[pl.ds(r - 2, C, stride=TL), :].astype(BF16)
        else:
            cells = down_ref[pl.ds((r - 10) * C, C), :]
        pick = ((row - 2 * r == lane) & (lane < 2)) | ((row - 32 - 2 * r == lane - (JL - 2)) & (lane >= JL - 2))
        total = total + dot(pick.astype(F32).astype(BF16), cells, ((1,), (1,)))
    head_ref[...] = total[:32].astype(BF16)
    tail_ref[...] = total[32:].astype(BF16)


def weights_kernel(w_ref, mix_ref, wt_ref, mixt_ref):
    wt_ref[...] = w_ref[...].T
    mixt_ref[...] = mix_ref[...].T


def legendre_kernel(
    place_ref, degree_ref, term_ref, lat_ref, fwd_hi, fwd_lo, inv_hi, inv_lo, left_ref, right_ref
):
    first = place_ref[0] * ORD
    order = (first + lax.broadcasted_iota(jnp.int32, (ORD, 128), 0)).astype(F32)
    squared = order * order
    term = term_ref[pl.ds(pl.multiple_of(first, ORD), ORD), :]
    cosines, seeds, undos = [], [], []
    for h in range(2):
        lanes = pl.ds(128 * h, 128)
        log_seed = term + order * lat_ref[pl.ds(1, 1), lanes]
        rescale = jnp.clip(-log_seed, 0.0, 80.0)
        cosines.append(jnp.broadcast_to(lat_ref[pl.ds(0, 1), lanes], (ORD, 128)))
        seeds.append(jnp.exp(log_seed + rescale))
        undos.append(jnp.exp(-rescale))
    refs = (left_ref, right_ref)

    def advance(degree, state):
        real = degree.astype(F32)
        below = real - 1.0
        a = degree_ref[0, degree] * lax.rsqrt(jnp.maximum(real * real - squared, 1.0))
        b = degree_ref[1, degree] * jnp.sqrt(jnp.maximum(below * below - squared, 0.0))
        found = []
        for h in range(2):
            last, before = state[2 * h], state[2 * h + 1]
            recurred = a * (cosines[h] * last - b * before)
            current = jnp.where(
                order == real, seeds[h], jnp.where(order < real, recurred, 0.0)
            )
            refs[h][pl.ds(pl.multiple_of(degree * ORD, ORD), ORD), :] = current * undos[h]
            found += [current, last]
        return tuple(found)

    empty = order * 0.0 * seeds[0]
    lax.fori_loop(0, LL, advance, (empty,) * 4, unroll=4)
    quad = lat_ref[pl.ds(2, 1), :]
    for m in range(ORD):
        table = jnp.concatenate(
            [left_ref[pl.ds(m, LL, stride=ORD), :], right_ref[pl.ds(m, LL, stride=ORD), :]], axis=1
        )
        fwd_hi[m], fwd_lo[m] = two_parts(table * quad)
        inv_hi[m], inv_lo[m] = two_parts(table.T)


def conv_kernel(
    dlat_ref,
    dlon_ref,
    basis_ref,
    quad_ref,
    x_ref,
    up_ref,
    down_ref,
    west_ref,
    east_ref,
    wt_ref,
    gain_ref,
    after_ref,
    normed_ref,
    shifted_ref,
    sums_ref,
    scaled_ref,
):
    row = lax.broadcasted_iota(jnp.int32, (64, JL), 0)
    lane = lax.broadcasted_iota(jnp.int32, (64, JL), 1)
    lanes = lax.broadcasted_iota(jnp.int32, (C, JL), 1)
    edges = jnp.concatenate([west_ref[...], east_ref[...]], axis=0).astype(F32).T.astype(BF16)
    for r in range(12):
        if r < 2:
            cells = up_ref[pl.ds(r * C, C), :].astype(F32)
        elif r < 10:
            cells = x_ref[pl.ds(r - 2, C, stride=TL), :]
        else:
            cells = down_ref[pl.ds((r - 10) * C, C), :].astype(F32)
        west = (row - 2 * r == lane - (JL - 2)) & (lane >= JL - 2)
        east = (row - 32 - 2 * r == lane) & (lane < 2)
        edge = dot(edges, (west | east).astype(F32).astype(BF16))
        for s in range(5):
            by = s - 2
            if by > 0:
                moved = pltpu.roll(jnp.where(lanes < by, edge, cells), JL - by, 1)
            elif by < 0:
                moved = pltpu.roll(jnp.where(lanes >= JL + by, edge, cells), -by, 1)
            else:
                moved = cells
            shifted_ref[s * 12 + r] = moved

    def one_row(t, carry):
        sums_ref[...] = jnp.zeros((NBASIS, C, JL), F32)
        for k in range(KSUP):
            b = basis_ref[t, k]
            place = (dlon_ref[t, k] + 2) * 12 + dlat_ref[t, k] + 2 + t
            sums_ref[b] = sums_ref[b] + quad_ref[t, k] * shifted_ref[place]
        aggregate = sums_ref[...].astype(BF16).reshape(NBASIS * C, JL)
        rows = pl.ds(t, C, stride=TL)
        after = x_ref[rows, :] + dot(wt_ref[...], aggregate)
        after_ref[rows, :] = after
        inverse = lax.rsqrt(jnp.sum(after * after, axis=0, keepdims=True) * (1.0 / C) + 1e-6)
        scaled_ref[rows, :] = after * inverse * gain_ref[...]
        return carry

    lax.fori_loop(0, TL, one_row, 0)
    normed_ref[...] = scaled_ref[...].astype(BF16)


def fourier_kernel(recv_ref, hi_ref, lo_ref, lane_ref, out_ref):
    circles = jnp.concatenate(
        [
            jnp.concatenate([recv_ref[8 * y + s] for s in range(8)], axis=1)
            for y in range(4)
        ],
        axis=0,
    )
    dims = ((1,), (1,))
    found = dot(hi_ref[...], circles, dims) + dot(lo_ref[...], circles, dims)
    out_ref[...] = dot(found.astype(BF16), lane_ref[...]).astype(BF16)


def spectral_kernel(
    recv_ref, fwd_hi, fwd_lo, inv_hi, inv_lo, filter_ref, out_ref, in_ref, rows_ref, back_ref
):
    m = pl.program_id(0)
    sign = (1 - 2 * (m % 2)).astype(F32)

    @pl.when(m == 0)
    def _():
        for j in range(3):
            in_ref[j] = recv_ref[:, 128 * j : 128 * (j + 1)].astype(F32)

    lane = lax.broadcasted_iota(jnp.int32, (8, 128), 1)
    parts = []
    for r in range(2):
        for j in range(3):
            near = in_ref[j, pl.ds(r * ORD + m, 8, stride=32), :]
            far = in_ref[j, pl.ds(256 + r * ORD + m, 8, stride=32), :]
            parts.append(near + sign * far)
    for yt in range(32):
        tile = None
        for n in range(6):
            moved = pltpu.roll(parts[n], (4 * n - 4 * yt) % 128, 1)
            tile = moved if tile is None else jnp.where(lane >= 4 * n, moved, tile)
        rows_ref[pl.ds(8 * yt, 8), :] = tile
    fields = rows_ref[...].astype(BF16)
    spectra = dot(fwd_hi[0], fields) + dot(fwd_lo[0], fields)
    filtered = (spectra * filter_ref[...]).astype(BF16)
    synthesis = dot(inv_hi[0], filtered) + dot(inv_lo[0], filtered)
    rows_ref[...] = synthesis
    found = [None] * 6
    for yt in range(32):
        tile = rows_ref[pl.ds(8 * yt, 8), :]
        for n in range(6):
            moved = pltpu.roll(tile, (4 * yt - 4 * n) % 128, 1)
            found[n] = moved if yt == 0 else jnp.where(lane >= 4 * yt, moved, found[n])
    for r in range(2):
        for j in range(3):
            value = found[3 * r + j]
            back_ref[j, pl.ds(r * ORD + m, 8, stride=32), :] = value
            back_ref[j, pl.ds(256 + r * ORD + m, 8, stride=32), :] = sign * value

    @pl.when(m == ORD - 1)
    def _():
        for j in range(3):
            out_ref[:, 128 * j : 128 * (j + 1)] = back_ref[j].astype(BF16)


def inverse_kernel(recv_ref, hi_ref, lo_ref, lane_ref, out_ref):
    turned = dot(lane_ref[...], recv_ref[...], ((1,), (1,))).astype(BF16)
    for s in range(8):
        lons = pl.ds(128 * s, 128)
        wave = dot(turned, hi_ref[:, lons]) + dot(turned, lo_ref[:, lons])
        act = jax.nn.gelu(wave, approximate=True).astype(BF16)
        for y in range(4):
            out_ref[8 * y + s] = act[96 * y : 96 * (y + 1)]


def mix_kernel(act_ref, after_ref, mixt_ref, out_ref, wide_ref):
    wide_ref[...] = act_ref[...].astype(F32)
    for t in range(TL):
        rows = pl.ds(t, C, stride=TL)
        mixed = dot(mixt_ref[...], wide_ref[rows, :].astype(BF16))
        out_ref[rows, :] = after_ref[rows, :] + mixed


def exchanged(blocks, axes):
    return lax.all_to_all(blocks, axes, split_axis=0, concat_axis=0, tiled=True)


def per_device(
    grid_field,
    disco_dlat,
    disco_dlon,
    disco_basis,
    disco_quad,
    disco_weight,
    norm_gain,
    spectral_filter,
    mix_weight,
):
    (fwd_hi, fwd_lo), (inv_hi, inv_lo) = longitude_tables()
    lanes = lane_order()
    smem = pl.BlockSpec(memory_space=pltpu.SMEM)
    vmem = pl.BlockSpec(memory_space=pltpu.VMEM)
    x = grid_field.reshape(C * TL, JL)

    lat_count = lax.axis_size(LAT)
    lon_count = lax.axis_size(LON)
    first, last = call(rows_kernel, "rows", (shape((2 * C, JL)), shape((2 * C, JL))))(x)
    up = lax.ppermute(last, LAT, [(i, i + 1) for i in range(lat_count - 1)])
    down = lax.ppermute(first, LAT, [(i + 1, i) for i in range(lat_count - 1)])
    head, tail = call(edges_kernel, "edges", (shape((32, C)), shape((32, C))))(x, up, down)
    west = lax.ppermute(tail, LON, [(i, (i + 1) % lon_count) for i in range(lon_count)])
    east = lax.ppermute(head, LON, [((i + 1) % lon_count, i) for i in range(lon_count)])

    wt, mixt = call(weights_kernel, "weights", (shape((C, NBASIS * C)), shape((C, C))))(
        disco_weight.reshape(NBASIS * C, C), mix_weight
    )
    place = lax.axis_index(RING).astype(jnp.int32).reshape(1)
    tables = call(
        legendre_kernel,
        "legendre",
        (shape((ORD, LL, NLAT)),) * 2 + (shape((ORD, NLAT, LL)),) * 2,
        in_specs=[smem, smem, vmem, vmem],
        scratch=(pltpu.VMEM((LL * ORD, 128), F32), pltpu.VMEM((LL * ORD, 128), F32)),
    )(place, degree_terms(), order_terms(), latitude_rows())
    own = lax.dynamic_slice_in_dim(spectral_filter, lax.axis_index(CHAN) * CB, CB, 0)
    own = jnp.concatenate([own, own, jnp.zeros((128 - 2 * CB, LL), F32)], axis=0).T
    gain = jnp.broadcast_to(norm_gain[:, None], (C, JL))

    after, normed = call(
        conv_kernel,
        "conv",
        (shape((C * TL, JL), F32), shape((C * TL, JL))),
        in_specs=[smem] * 4 + [vmem] * 7,
        scratch=(
            pltpu.VMEM((60, C, JL), F32),
            pltpu.VMEM((NBASIS, C, JL), F32),
            pltpu.VMEM((C * TL, JL), F32),
        ),
    )(disco_dlat, disco_dlon, disco_basis, disco_quad, x, up, down, west, east, wt, gain)

    portion = exchanged(normed.reshape(32, CB * TL, JL), CHAN)
    fourier = call(fourier_kernel, "fourier", shape((2 * MM, C)))(portion, fwd_hi, fwd_lo, lanes)
    gathered = exchanged(fourier.reshape(16, 2 * ORD, C), RING)
    whole = pl.BlockSpec((2 * MM, C), lambda m: (0, 0))
    table = pl.BlockSpec((1, LL, NLAT), lambda m: (m, 0, 0))
    synthesis = call(
        spectral_kernel,
        "spectral",
        shape((2 * MM, C)),
        grid=(ORD,),
        in_specs=[whole] + [table] * 4 + [pl.BlockSpec((LL, 128), lambda m: (0, 0))],
        out_specs=whole,
        scratch=(
            pltpu.VMEM((3, 2 * MM, 128), F32),
            pltpu.VMEM((NLAT, 128), F32),
            pltpu.VMEM((3, 2 * MM, 128), F32),
        ),
    )(gathered.reshape(2 * MM, C), *tables, own)
    returned = exchanged(synthesis.reshape(16, 2 * ORD, C), RING)
    activated = call(inverse_kernel, "inverse", shape((32, CB * TL, JL)))(
        returned.reshape(2 * MM, C), inv_hi, inv_lo, lanes
    )
    mixed = exchanged(activated, CHAN)
    out = call(
        mix_kernel, "mix", shape((C * TL, JL), F32), scratch=(pltpu.VMEM((C * TL, JL), F32),)
    )(mixed.reshape(C * TL, JL), after, mixt)
    return out.reshape(C, TL, JL)


def solution(mesh):
    torus = Mesh(mesh.devices.reshape(8, 4, 2, 4, 2), ("zl", "y", "zh", "x", "core"))
    placed = (P(None, LAT, LON),) + (P(LAT, None),) * 4 + (P(),) * 4
    return jax.shard_map(
        per_device, mesh=torus, in_specs=placed, out_specs=P(None, LAT, LON), check_vma=False
    )
```

time: 801 us -> 198 us (0.25)
  the two profiles are of different devices: /device:TPU:32 before, /device:TPU:1 now
where the time goes in v1:
time: 198 us; the launch traced here: 197 us
  blocking collectives  101 us (51%)
  Pallas kernels  61.3 us (31%)
  starting transfers between devices  18.5 us (9%)
  waiting for transfers between devices  13.1 us (7%)
  local copies, waits for them, and re-layouts  2.45 us (1%)
    all_to_all x3, blocking collectives, exchanged(): return lax.all_to_all(blocks, axes, split_axis=0, concat_axis=0, tiled=True)  101 us
    pallas_call x1, Pallas kernels, per_device(): call(spectral_kernel, 'spectral', shape((2 * MM, C)), grid=(ORD,), in_spe...  17.4 us
    pallas_call x1, Pallas kernels, per_device(): call(conv_kernel, 'conv', (shape((C * TL, JL), F32), shape((C * TL, JL)))...  14.3 us
    pallas_call x1, Pallas kernels, per_device(): call(legendre_kernel, 'legendre', (shape((ORD, LL, NLAT)),) * 2 + (shape(...  8.97 us
    all_to_all x1, waiting for transfers between devices, exchanged(): return lax.all_to_all(blocks, axes, split_axis=0, concat_axis=0, tiled=True)  7.79 us
    ppermute x1, starting transfers between devices, per_device(): lax.ppermute(tail, LON, [(i, (i + 1) % lon_count) for i in range(lon_coun...  5.79 us
    pallas_call x1, Pallas kernels, per_device(): call(inverse_kernel, 'inverse', shape((32, CB * TL, JL)))  4.81 us
    all_to_all x1, starting transfers between devices, exchanged(): return lax.all_to_all(blocks, axes, split_axis=0, concat_axis=0, tiled=True)  4.14 us
  transfers between devices with their start and end apart: 5, of which 3 were waited for; matrix products, arithmetic and copies ran while one was open for 0% of the time, Pallas kernels for 6%

profile of v1, /device:TPU:1, one launch (start us, length us, event | category | flops | bytes accessed | tf_op | source)
XLA Modules:
  0.0 196.8 jit_solution(888498567861951574)
XLA Ops:
  0.0 0.0 copy-start
  0.0 2.3 %rows.1 = (bf16[768,128]{1,0:T(8,128)(2,1)}, bf16[768,128]{1,0:T(8,128)(2,1)}) custom-call(f32[3072,128]{1,0:T(8,128)} %bitcast.12), custom_call_target="tpu_custom_call" | custom-call | tf_op jit(solution)/shard_map/rows/pallas_call | solution.py:351
  2.3 4.0 %collective-permute-start = (bf16[768,128]{1,0:T(8,128)(2,1)}, bf16[768,128]{1,0:T(8,128)(2,1)S(1)}, u32[]{:S(2)}, u32[]{:S(2)}) collective-permute-start(bf16[768,128]{1,0:T(8,128)(2,1)} %get-tuple-element.17), channel_id=1, source_target_pairs={{0,16},{16,32},{32,48},{48,64},{64,80},{80,96},{96,112},{112,128},... | collective-permute-start | bytes 589832 | tf_op jit(solution)/shard_map/ppermute | solution.py:352
  6.3 0.0 copy-start.6
  6.4 1.3 collective-permute-start.1
  7.7 1.6 collective-permute-done.up_ref
  9.3 3.7 %collective-permute-done.1.down_ref = bf16[768,128]{1,0:T(8,128)(2,1)S(1)} collective-permute-done((bf16[768,128]{1,0:T(8,128)(2,1)}, bf16[768,128]{1,0:T(8,128)(2,1)S(1)}, u32[]{:S(2)}, u32[]{:S(2)}) %collective-permute-start.1) | collective-permute-done | bytes 196640 | tf_op jit(solution)/shard_map/ppermute | solution.py:353
  13.0 0.7 copy-done.3
  13.7 2.8 %edges.1 = (bf16[32,384]{1,0:T(8,128)(2,1)}, bf16[32,384]{1,0:T(8,128)(2,1)}) custom-call(f32[3072,128]{1,0:T(8,128)} %bitcast.13, bf16[768,128]{1,0:T(8,128)(2,1)} %copy-done.2, bf16[768,128]{1,0:T(8,128)(2,1)} %copy-done.3), custom_call_target="tpu_custom_call" | custom-call | tf_op jit(solution)/shard_map/edges/pallas_call | solution.py:354
  16.5 5.8 %collective-permute-start.2 = (bf16[32,384]{1,0:T(8,128)(2,1)}, bf16[32,384]{1,0:T(8,128)(2,1)S(1)}, u32[]{:S(2)}, u32[]{:S(2)}) collective-permute-start(bf16[32,384]{1,0:T(8,128)(2,1)} %get-tuple-element.19), channel_id=1, source_target_pairs={{0,1},{1,2},{2,3},{3,4},{4,5},{5,6},{6,7},{7,8},{8,9},{9,10},{10,1... | collective-permute-start | bytes 73736 | tf_op jit(solution)/shard_map/ppermute | solution.py:355
  22.3 3.3 %collective-permute-start.3 = (bf16[32,384]{1,0:T(8,128)(2,1)}, bf16[32,384]{1,0:T(8,128)(2,1)S(1)}, u32[]{:S(2)}, u32[]{:S(2)}) collective-permute-start(bf16[32,384]{1,0:T(8,128)(2,1)} %get-tuple-element.20), channel_id=1, source_target_pairs={{1,0},{2,1},{3,2},{4,3},{5,4},{6,5},{7,6},{8,7},{9,8},{10,9},{11,1... | collective-permute-start | bytes 73736 | tf_op jit(solution)/shard_map/ppermute | solution.py:356
  25.6 2.8 %weights.1 = (bf16[384,1536]{1,0:T(8,128)(2,1)}, bf16[384,384]{1,0:T(8,128)(2,1)}) custom-call(bf16[1536,384]{1,0:T(8,128)(2,1)} %bitcast.20, bf16[384,384]{1,0:T(8,128)(2,1)} %mix_ref.1), custom_call_target="tpu_custom_call" | custom-call | tf_op jit(solution)/shard_map/weights/pallas_call | solution.py:358
  28.4 0.0 collective-permute-done.2.west_ref
  28.4 0.0 collective-permute-done.3.east_ref
  28.4 0.0 copy-done.6
  28.4 0.0 copy-start.5
  28.4 0.8 broadcast_in_dim.4.gain_ref
  29.2 14.3 %conv.1 = (f32[3072,128]{1,0:T(8,128)}, bf16[3072,128]{1,0:T(8,128)(2,1)}) custom-call(s32[8,16]{1,0:T(8,128)} %dlat_ref.1, s32[8,16]{1,0:T(8,128)} %dlon_ref.1, s32[8,16]{1,0:T(8,128)} %basis_ref.1, f32[8,16]{1,0:T(8,128)} %quad_ref.1, f32[3072,128]{1,0:T(8,128)} %bitcast.14, bf16[768,128]{1,0:T(8,128)(2,1)} %copy-done.2, bf16[768,128]{1,0:T(8,128)(2,1)} %copy-done.3, ...), custom_call_target="tpu_custom_call" | custom-call | tf_op jit(solution)/shard_map/conv/pallas_call | solution.py:373
  43.5 44.8 %all_to_all.20.recv_ref = bf16[32,96,128]{2,1,0:T(8,128)(2,1)} all-to-all(bf16[32,96,128]{2,1,0:T(8,128)(2,1)} %bitcast.21), channel_id=1, replica_groups=mesh['zl'=8,'y'=4,'zh'=2,'x'=4,'core'=2] {'y','x','core'}, dimensions={0} | all-to-all | bytes 1572864 | tf_op jit(solution)/shard_map/all_to_all | solution.py:329
  88.4 4.1 %fourier.1 = bf16[512,384]{1,0:T(8,128)(2,1)} custom-call(bf16[32,96,128]{2,1,0:T(8,128)(2,1)} %all_to_all.20.recv_ref, bf16[512,1024]{1,0:T(8,128)(2,1)} %constant.51.clone.hi_ref, bf16[512,1024]{1,0:T(8,128)(2,1)} %constant.52.clone.lo_ref, bf16[384,384]{1,0:T(8,128)(2,1)} %constant.53.clone.lane_ref), custom_call_target="tpu_custom_call" | custom-call | tf_op jit(solution)/shard_map/fourier/pallas_call | solution.py:386
  92.5 4.1 %all-to-all-start.1 = ((bf16[16,32,384]{2,1,0:T(8,128)(2,1)}), bf16[16,32,384]{2,1,0:T(8,128)(2,1)S(1)}, u32[]{:S(2)}, u32[]{:S(2)}) async-start(bf16[16,32,384]{2,1,0:T(8,128)(2,1)} %bitcast.18), calls=%async_computation.1 | async-start | bytes 786432 | tf_op jit(solution)/shard_map/all_to_all | solution.py:329
  96.7 0.1 copy.19
  96.8 0.1 pad.2.clone
  96.9 9.0 %legendre.1 = (bf16[16,256,256]{2,1,0:T(8,128)(2,1)}, bf16[16,256,256]{2,1,0:T(8,128)(2,1)}, bf16[16,256,256]{2,1,0:T(8,128)(2,1)}, bf16[16,256,256]{2,1,0:T(8,128)(2,1)}) custom-call(s32[1]{0:T(128)} %bitcast.5.place_ref, f32[2,256]{1,0:T(2,128)} %constant.48.clone.degree_ref, f32[256,128]{1,0:T(8,128)} %constant.49.clone.term_ref, ...), custom_call_target="tpu_custom_call" | custom-call | tf_op jit(solution)/shard_map/legendre/pallas_call | solution.py:362
  105.8 0.7 maximum_bitcast_fusion.filter_ref
  106.6 7.8 %all-to-all-done.1 = bf16[16,32,384]{2,1,0:T(8,128)(2,1)S(1)} async-done(((bf16[16,32,384]{2,1,0:T(8,128)(2,1)}), bf16[16,32,384]{2,1,0:T(8,128)(2,1)S(1)}, u32[]{:S(2)}, u32[]{:S(2)}) %all-to-all-start.1) | async-done | bytes 393248 | tf_op jit(solution)/shard_map/all_to_all | solution.py:329
  114.4 0.7 copy-done.1
  115.1 17.4 %spectral.1 = bf16[512,384]{1,0:T(8,128)(2,1)} custom-call(bf16[512,384]{1,0:T(8,128)(2,1)} %bitcast.16, bf16[16,256,256]{2,1,0:T(8,128)(2,1)} %get-tuple-element.23.fwd_hi, bf16[16,256,256]{2,1,0:T(8,128)(2,1)} %get-tuple-element.24.fwd_lo, bf16[16,256,256]{2,1,0:T(8,128)(2,1)} %get-tuple-element.25.inv_hi, bf16[16,256,256]{2,1,0:T(8,128)(2,1)} %get-tuple-element.26.inv_lo, ...), custom_call_target="tpu_custom_call" | custom-call | tf_op jit(solution)/shard_map/spectral/pallas_call | solution.py:390
  132.5 30.2 %all_to_all.21 = bf16[16,32,384]{2,1,0:T(8,128)(2,1)} all-to-all(bf16[16,32,384]{2,1,0:T(8,128)(2,1)} %bitcast.17), channel_id=1, replica_groups=mesh['zl'=8,'y'=4,'zh'=2,'x'=4,'core'=2] {'zh','zl'}, dimensions={0} | all-to-all | bytes 786432 | tf_op jit(solution)/shard_map/all_to_all | solution.py:329
  162.7 4.8 %inverse.1 = bf16[32,96,128]{2,1,0:T(8,128)(2,1)} custom-call(bf16[512,384]{1,0:T(8,128)(2,1)} %bitcast.19, bf16[512,1024]{1,0:T(8,128)(2,1)} %constant.54.clone.hi_ref, bf16[512,1024]{1,0:T(8,128)(2,1)} %constant.55.clone.lo_ref, bf16[384,384]{1,0:T(8,128)(2,1)} %constant.53.clone.lane_ref), custom_call_target="tpu_custom_call" | custom-call | tf_op jit(solution)/shard_map/inverse/pallas_call | solution.py:404
  167.5 25.5 %all_to_all.22 = bf16[32,96,128]{2,1,0:T(8,128)(2,1)} all-to-all(bf16[32,96,128]{2,1,0:T(8,128)(2,1)} %inverse.1), channel_id=1, replica_groups=mesh['zl'=8,'y'=4,'zh'=2,'x'=4,'core'=2] {'y','x','core'}, dimensions={0} | all-to-all | bytes 1572864 | tf_op jit(solution)/shard_map/all_to_all | solution.py:329
  193.0 3.8 %mix.1 = f32[3072,128]{1,0:T(8,128)} custom-call(bf16[3072,128]{1,0:T(8,128)(2,1)} %bitcast.15, f32[3072,128]{1,0:T(8,128)} %get-tuple-element.27.after_ref, bf16[384,384]{1,0:T(8,128)(2,1)} %get-tuple-element.28.mixt_ref), custom_call_target="tpu_custom_call" | custom-call | tf_op jit(solution)/shard_map/mix/pallas_call | solution.py:408
  (10 shorter events, 0.0 us)
Async XLA Ops:
  0.0 96.6 %copy-start = (f32[384,256]{1,0:T(8,128)S(1)}, f32[384,256]{1,0:T(8,128)}, u32[]{:S(2)}) copy-start(f32[384,256]{1,0:T(8,128)} %param.24) | copy-start | bytes 1179652
  2.3 6.9 %collective-permute-start = (bf16[768,128]{1,0:T(8,128)(2,1)}, bf16[768,128]{1,0:T(8,128)(2,1)S(1)}, u32[]{:S(2)}, u32[]{:S(2)}) collective-permute-start(bf16[768,128]{1,0:T(8,128)(2,1)} %get-tuple-element.17), channel_id=1, source_target_pairs={{0,16},{16,32},{32,48},{48,64},{64,80},{80,96},{96,112},{112,128},... | collective-permute-start | bytes 589832 | tf_op jit(solution)/shard_map/ppermute | solution.py:352
  6.3 22.0 %copy-start.6 = (f32[384]{0:T(512)S(1)}, f32[384]{0:T(512)}, u32[]{:S(2)}) copy-start(f32[384]{0:T(512)} %param.23) | copy-start | bytes 4612
  6.4 6.6 %collective-permute-start.1 = (bf16[768,128]{1,0:T(8,128)(2,1)}, bf16[768,128]{1,0:T(8,128)(2,1)S(1)}, u32[]{:S(2)}, u32[]{:S(2)}) collective-permute-start(bf16[768,128]{1,0:T(8,128)(2,1)} %get-tuple-element.18), channel_id=1, source_target_pairs={{16,0},{32,16},{48,32},{64,48},{80,64},{96,80},{112,96},{128,112},... | collective-permute-start | bytes 589832 | tf_op jit(solution)/shard_map/ppermute | solution.py:353
  9.3 3.7 %copy-start.2 = (bf16[768,128]{1,0:T(8,128)(2,1)}, bf16[768,128]{1,0:T(8,128)(2,1)S(1)}, u32[]{:S(2)}) copy-start(bf16[768,128]{1,0:T(8,128)(2,1)S(1)} %collective-permute-done.up_ref) | copy-start | bytes 589828
  13.0 0.7 copy-start.3
  16.5 11.9 %collective-permute-start.2 = (bf16[32,384]{1,0:T(8,128)(2,1)}, bf16[32,384]{1,0:T(8,128)(2,1)S(1)}, u32[]{:S(2)}, u32[]{:S(2)}) collective-permute-start(bf16[32,384]{1,0:T(8,128)(2,1)} %get-tuple-element.19), channel_id=1, source_target_pairs={{0,1},{1,2},{2,3},{3,4},{4,5},{5,6},{6,7},{7,8},{8,9},{9,10},{10,1... | collective-permute-start | bytes 73736 | tf_op jit(solution)/shard_map/ppermute | solution.py:355
  22.3 6.1 %collective-permute-start.3 = (bf16[32,384]{1,0:T(8,128)(2,1)}, bf16[32,384]{1,0:T(8,128)(2,1)S(1)}, u32[]{:S(2)}, u32[]{:S(2)}) collective-permute-start(bf16[32,384]{1,0:T(8,128)(2,1)} %get-tuple-element.20), channel_id=1, source_target_pairs={{1,0},{2,1},{3,2},{4,3},{5,4},{6,5},{7,6},{8,7},{9,8},{10,9},{11,1... | collective-permute-start | bytes 73736 | tf_op jit(solution)/shard_map/ppermute | solution.py:356
  28.4 0.8 copy-start.4
  28.4 0.8 copy-start.5
  92.5 21.9 %all-to-all-start.1 = ((bf16[16,32,384]{2,1,0:T(8,128)(2,1)}), bf16[16,32,384]{2,1,0:T(8,128)(2,1)S(1)}, u32[]{:S(2)}, u32[]{:S(2)}) async-start(bf16[16,32,384]{2,1,0:T(8,128)(2,1)} %bitcast.18), calls=%async_computation.1 | async-start | bytes 786432 | tf_op jit(solution)/shard_map/all_to_all | solution.py:329
  114.4 0.7 copy-start.1

commit v2 on v1

--- a/solution.py
+++ b/solution.py
@@ -20,6 +20,7 @@
 JL = 128
 CB = 12
 ORD = 16
+STEP = 4
 LAT = ("zl", "y")
 LON = ("zh", "x", "core")
 CHAN = ("y", "x", "core")
@@ -28,7 +29,7 @@
 BF16 = jnp.bfloat16
 
 
-def call(kernel, name, out_shape, in_specs=None, scratch=(), grid=None, out_specs=None):
+def call(kernel, name, mib, out_shape, in_specs=None, scratch=(), grid=None, out_specs=None):
     kwargs = {}
     if grid is not None:
         kwargs["grid"] = grid
@@ -41,7 +42,7 @@
         out_shape=out_shape,
         scratch_shapes=list(scratch),
         name=name,
-        compiler_params=pltpu.CompilerParams(vmem_limit_bytes=60 * 1024 * 1024),
+        compiler_params=pltpu.CompilerParams(vmem_limit_bytes=mib * 1024 * 1024),
         **kwargs,
     )
 
@@ -121,7 +122,7 @@
         last_ref[pl.ds(u * C, C), :] = x_ref[pl.ds(TL - 2 + u, C, stride=TL), :].astype(BF16)
 
 
-def edges_kernel(x_ref, up_ref, down_ref, head_ref, tail_ref):
+def edges_kernel(core_ref, x_ref, up_ref, down_ref, far_ref, near_ref):
     row = lax.broadcasted_iota(jnp.int32, (64, JL), 0)
     lane = lax.broadcasted_iota(jnp.int32, (64, JL), 1)
     total = jnp.zeros((64, C), F32)
@@ -132,19 +133,22 @@
             cells = x_ref[pl.ds(r - 2, C, stride=TL), :].astype(BF16)
         else:
             cells = down_ref[pl.ds((r - 10) * C, C), :]
-        pick = ((row - 2 * r == lane) & (lane < 2)) | ((row - 32 - 2 * r == lane - (JL - 2)) & (lane >= JL - 2))
-        total = total + dot(pick.astype(F32).astype(BF16), cells, ((1,), (1,)))
-    head_ref[...] = total[:32].astype(BF16)
-    tail_ref[...] = total[32:].astype(BF16)
-
-
-def weights_kernel(w_ref, mix_ref, wt_ref, mixt_ref):
+        head = (row - 2 * r == lane) & (lane < 2)
+        tail = (row - 32 - 2 * r == lane - (JL - 2)) & (lane >= JL - 2)
+        total = total + dot((head | tail).astype(F32).astype(BF16), cells, ((1,), (1,)))
+    odd = core_ref[0] == 1
+    far_ref[...] = jnp.where(odd, total[32:], total[:32]).astype(BF16)
+    near_ref[...] = jnp.where(odd, total[:32], total[32:]).astype(BF16)
+
+
+def weights_kernel(w_ref, mix_ref, norm_ref, wt_ref, mixt_ref, gain_ref):
+    gain_ref[...] = jnp.broadcast_to(norm_ref[...], (JL, C)).T
     wt_ref[...] = w_ref[...].T
     mixt_ref[...] = mix_ref[...].T
 
 
 def legendre_kernel(
-    place_ref, degree_ref, term_ref, lat_ref, fwd_hi, fwd_lo, inv_hi, inv_lo, left_ref, right_ref
+    place_ref, degree_ref, term_ref, lat_ref, table_ref, left_ref, right_ref
 ):
     first = place_ref[0] * ORD
     order = (first + lax.broadcasted_iota(jnp.int32, (ORD, 128), 0)).astype(F32)
@@ -183,8 +187,8 @@
         table = jnp.concatenate(
             [left_ref[pl.ds(m, LL, stride=ORD), :], right_ref[pl.ds(m, LL, stride=ORD), :]], axis=1
         )
-        fwd_hi[m], fwd_lo[m] = two_parts(table * quad)
-        inv_hi[m], inv_lo[m] = two_parts(table.T)
+        table_ref[0, m], table_ref[1, m] = two_parts(table * quad)
+        table_ref[2, m], table_ref[3, m] = two_parts(table.T)
 
 
 def conv_kernel(
@@ -195,20 +199,12 @@
     x_ref,
     up_ref,
     down_ref,
-    west_ref,
-    east_ref,
     wt_ref,
-    gain_ref,
     after_ref,
-    normed_ref,
     shifted_ref,
     sums_ref,
-    scaled_ref,
 ):
-    row = lax.broadcasted_iota(jnp.int32, (64, JL), 0)
-    lane = lax.broadcasted_iota(jnp.int32, (64, JL), 1)
     lanes = lax.broadcasted_iota(jnp.int32, (C, JL), 1)
-    edges = jnp.concatenate([west_ref[...], east_ref[...]], axis=0).astype(F32).T.astype(BF16)
     for r in range(12):
         if r < 2:
             cells = up_ref[pl.ds(r * C, C), :].astype(F32)
@@ -216,15 +212,12 @@
             cells = x_ref[pl.ds(r - 2, C, stride=TL), :]
         else:
             cells = down_ref[pl.ds((r - 10) * C, C), :].astype(F32)
-        west = (row - 2 * r == lane - (JL - 2)) & (lane >= JL - 2)
-        east = (row - 32 - 2 * r == lane) & (lane < 2)
-        edge = dot(edges, (west | east).astype(F32).astype(BF16))
         for s in range(5):
             by = s - 2
             if by > 0:
-                moved = pltpu.roll(jnp.where(lanes < by, edge, cells), JL - by, 1)
+                moved = jnp.where(lanes < JL - by, pltpu.roll(cells, JL - by, 1), 0.0)
             elif by < 0:
-                moved = pltpu.roll(jnp.where(lanes >= JL + by, edge, cells), -by, 1)
+                moved = jnp.where(lanes >= -by, pltpu.roll(cells, -by, 1), 0.0)
             else:
                 moved = cells
             shifted_ref[s * 12 + r] = moved
@@ -237,13 +230,77 @@
             sums_ref[b] = sums_ref[b] + quad_ref[t, k] * shifted_ref[place]
         aggregate = sums_ref[...].astype(BF16).reshape(NBASIS * C, JL)
         rows = pl.ds(t, C, stride=TL)
-        after = x_ref[rows, :] + dot(wt_ref[...], aggregate)
+        after_ref[rows, :] = x_ref[rows, :] + dot(wt_ref[...], aggregate)
+        return carry
+
+    lax.fori_loop(0, TL, one_row, 0)
+
+
+def seam_kernel(
+    core_ref,
+    dlat_ref,
+    dlon_ref,
+    basis_ref,
+    quad_ref,
+    inner_ref,
+    far_ref,
+    near_ref,
+    wt_ref,
+    gain_ref,
+    after_ref,
+    normed_ref,
+    scaled_ref,
+):
+    even = core_ref[0] == 0
+    far = far_ref[...].astype(F32)
+    near = near_ref[...].astype(F32)
+    west = jnp.where(even, far, near)
+    east = jnp.where(even, near, far)
+    edges = jnp.concatenate([west, east], axis=0).T.astype(BF16)
+    row = lax.broadcasted_iota(jnp.int32, (64, 128), 0)
+    lane = lax.broadcasted_iota(jnp.int32, (8, 128), 1)
+    own = (lane >> 2) & 7
+    col = lane & 3
+    gather = jnp.zeros((64, 128), F32)
+    for k in range(KSUP):
+        dlat = jnp.zeros((8, 128), jnp.int32)
+        dlon = dlat
+        basis = dlat
+        quad = jnp.zeros((8, 128), F32)
+        for t in range(TL):
+            here = own == t
+            dlat = jnp.where(here, dlat_ref[t, k], dlat)
+            dlon = jnp.where(here, dlon_ref[t, k], dlon)
+            basis = jnp.where(here, basis_ref[t, k], basis)
+            quad = jnp.where(here, quad_ref[t, k], quad)
+        start = 2 * (own + 2 + dlat)
+        cell = col + dlon
+        source = jnp.where(
+            col < 2,
+            jnp.where(cell >= 2, 32 + start + cell - 2, -1),
+            jnp.where(cell < 2, start + cell, -1),
+        )
+        source = jnp.where(basis == lane >> 5, source, -1)
+        gather = gather + jnp.where(
+            row == jnp.concatenate([source] * 8, axis=0), jnp.concatenate([quad] * 8, axis=0), 0.0
+        )
+    high, low = two_parts(gather)
+    sums = dot(edges, high) + dot(edges, low)
+    aggregate = jnp.concatenate(
+        [sums.astype(BF16)]
+        + [pltpu.roll(sums, 128 - 32 * b, 1).astype(BF16) for b in range(1, NBASIS)],
+        axis=0,
+    )
+    seam = dot(wt_ref[...], aggregate)
+    lanes = lax.broadcasted_iota(jnp.int32, (C, JL), 1)
+    outer = (lanes < 2) | (lanes >= JL - 2)
+    for t in range(TL):
+        rows = pl.ds(t, C, stride=TL)
+        moved = pltpu.roll(seam, (JL - 2 - 4 * t) % JL, 1)
+        after = inner_ref[rows, :] + jnp.where(outer, moved, 0.0)
         after_ref[rows, :] = after
         inverse = lax.rsqrt(jnp.sum(after * after, axis=0, keepdims=True) * (1.0 / C) + 1e-6)
         scaled_ref[rows, :] = after * inverse * gain_ref[...]
-        return carry
-
-    lax.fori_loop(0, TL, one_row, 0)
     normed_ref[...] = scaled_ref[...].astype(BF16)
 
 
@@ -261,47 +318,52 @@
 
 
 def spectral_kernel(
-    recv_ref, fwd_hi, fwd_lo, inv_hi, inv_lo, filter_ref, out_ref, in_ref, rows_ref, back_ref
+    recv_ref, table_ref, filter_ref, out_ref, in_ref, rows_ref, back_ref
 ):
-    m = pl.program_id(0)
-    sign = (1 - 2 * (m % 2)).astype(F32)
-
-    @pl.when(m == 0)
+    first = pl.program_id(0) * STEP
+
+    @pl.when(first == 0)
     def _():
         for j in range(3):
             in_ref[j] = recv_ref[:, 128 * j : 128 * (j + 1)].astype(F32)
 
     lane = lax.broadcasted_iota(jnp.int32, (8, 128), 1)
-    parts = []
-    for r in range(2):
-        for j in range(3):
-            near = in_ref[j, pl.ds(r * ORD + m, 8, stride=32), :]
-            far = in_ref[j, pl.ds(256 + r * ORD + m, 8, stride=32), :]
-            parts.append(near + sign * far)
-    for yt in range(32):
-        tile = None
-        for n in range(6):
-            moved = pltpu.roll(parts[n], (4 * n - 4 * yt) % 128, 1)
-            tile = moved if tile is None else jnp.where(lane >= 4 * n, moved, tile)
-        rows_ref[pl.ds(8 * yt, 8), :] = tile
-    fields = rows_ref[...].astype(BF16)
-    spectra = dot(fwd_hi[0], fields) + dot(fwd_lo[0], fields)
-    filtered = (spectra * filter_ref[...]).astype(BF16)
-    synthesis = dot(inv_hi[0], filtered) + dot(inv_lo[0], filtered)
-    rows_ref[...] = synthesis
-    found = [None] * 6
-    for yt in range(32):
-        tile = rows_ref[pl.ds(8 * yt, 8), :]
-        for n in range(6):
-            moved = pltpu.roll(tile, (4 * yt - 4 * n) % 128, 1)
-            found[n] = moved if yt == 0 else jnp.where(lane >= 4 * yt, moved, found[n])
-    for r in range(2):
-        for j in range(3):
-            value = found[3 * r + j]
-            back_ref[j, pl.ds(r * ORD + m, 8, stride=32), :] = value
-            back_ref[j, pl.ds(256 + r * ORD + m, 8, stride=32), :] = sign * value
-
-    @pl.when(m == ORD - 1)
+    for i in range(STEP):
+        parts = []
+        for r in range(2):
+            for j in range(3):
+                near = in_ref[j, pl.ds(r * ORD + first + i, 8, stride=32), :]
+                far = in_ref[j, pl.ds(256 + r * ORD + first + i, 8, stride=32), :]
+                parts.append(near - far if i % 2 else near + far)
+        for yt in range(32):
+            tile = None
+            for n in range(6):
+                moved = pltpu.roll(parts[n], (4 * n - 4 * yt) % 128, 1)
+                tile = moved if tile is None else jnp.where(lane >= 4 * n, moved, tile)
+            rows_ref[i, pl.ds(8 * yt, 8), :] = tile
+    filtered = []
+    for i in range(STEP):
+        fields = rows_ref[i].astype(BF16)
+        spectra = dot(table_ref[0, i], fields) + dot(table_ref[1, i], fields)
+        filtered.append((spectra * filter_ref[...]).astype(BF16))
+    for i in range(STEP):
+        rows_ref[i] = dot(table_ref[2, i], filtered[i]) + dot(table_ref[3, i], filtered[i])
+    for i in range(STEP):
+        found = [None] * 6
+        for yt in range(32):
+            tile = rows_ref[i, pl.ds(8 * yt, 8), :]
+            for n in range(6):
+                moved = pltpu.roll(tile, (4 * yt - 4 * n) % 128, 1)
+                found[n] = moved if yt == 0 else jnp.where(lane >= 4 * yt, moved, found[n])
+        for r in range(2):
+            for j in range(3):
+                value = found[3 * r + j]
+                back_ref[j, pl.ds(r * ORD + first + i, 8, stride=32), :] = value
+                back_ref[j, pl.ds(256 + r * ORD + first + i, 8, stride=32), :] = (
+                    -value if i % 2 else value
+                )
+
+    @pl.when(first == ORD - STEP)
     def _():
         for j in range(3):
             out_ref[:, 128 * j : 128 * (j + 1)] = back_ref[j].astype(BF16)
@@ -327,6 +389,11 @@
 
 def exchanged(blocks, axes):
     return lax.all_to_all(blocks, axes, split_axis=0, concat_axis=0, tiled=True)
+
+
+def pairs(count, first):
+    ends = [(i, (i + 1) % count) for i in range(first, count, 2)]
+    return ends + [(j, i) for i, j in ends]
 
 
 def per_device(
@@ -348,65 +415,74 @@
 
     lat_count = lax.axis_size(LAT)
     lon_count = lax.axis_size(LON)
-    first, last = call(rows_kernel, "rows", (shape((2 * C, JL)), shape((2 * C, JL))))(x)
+    first, last = call(rows_kernel, "rows", 6, (shape((2 * C, JL)), shape((2 * C, JL))))(x)
     up = lax.ppermute(last, LAT, [(i, i + 1) for i in range(lat_count - 1)])
     down = lax.ppermute(first, LAT, [(i + 1, i) for i in range(lat_count - 1)])
-    head, tail = call(edges_kernel, "edges", (shape((32, C)), shape((32, C))))(x, up, down)
-    west = lax.ppermute(tail, LON, [(i, (i + 1) % lon_count) for i in range(lon_count)])
-    east = lax.ppermute(head, LON, [((i + 1) % lon_count, i) for i in range(lon_count)])
-
-    wt, mixt = call(weights_kernel, "weights", (shape((C, NBASIS * C)), shape((C, C))))(
-        disco_weight.reshape(NBASIS * C, C), mix_weight
-    )
+    wt, mixt, gain = call(
+        weights_kernel,
+        "weights",
+        10,
+        (shape((C, NBASIS * C)), shape((C, C)), shape((C, JL), F32)),
+    )(disco_weight.reshape(NBASIS * C, C), mix_weight, norm_gain.reshape(1, C))
+    own = lax.dynamic_slice_in_dim(spectral_filter, lax.axis_index(CHAN) * CB, CB, 0)
+    own = jnp.concatenate([own, own, jnp.zeros((128 - 2 * CB, LL), F32)], axis=0).T
+    up, down, wt, mixt, gain, own = lax.optimization_barrier((up, down, wt, mixt, gain, own))
+    core = lax.axis_index("core").astype(jnp.int32).reshape(1)
+    far, near = call(
+        edges_kernel, "edges", 6, (shape((32, C)), shape((32, C))), in_specs=[smem] + [vmem] * 3
+    )(core, x, up, down)
+    far = lax.ppermute(far, LON, pairs(lon_count, 1))
+    near = lax.ppermute(near, LON, pairs(lon_count, 0))
+
     place = lax.axis_index(RING).astype(jnp.int32).reshape(1)
     tables = call(
         legendre_kernel,
-        "legendre",
-        (shape((ORD, LL, NLAT)),) * 2 + (shape((ORD, NLAT, LL)),) * 2,
+        "legendre", 57,
+        shape((4, ORD, LL, NLAT)),
         in_specs=[smem, smem, vmem, vmem],
         scratch=(pltpu.VMEM((LL * ORD, 128), F32), pltpu.VMEM((LL * ORD, 128), F32)),
     )(place, degree_terms(), order_terms(), latitude_rows())
-    own = lax.dynamic_slice_in_dim(spectral_filter, lax.axis_index(CHAN) * CB, CB, 0)
-    own = jnp.concatenate([own, own, jnp.zeros((128 - 2 * CB, LL), F32)], axis=0).T
-    gain = jnp.broadcast_to(norm_gain[:, None], (C, JL))
-
+
+    inner = call(
+        conv_kernel,
+        "conv", 24,
+        shape((C * TL, JL), F32),
+        in_specs=[smem] * 4 + [vmem] * 4,
+        scratch=(pltpu.VMEM((60, C, JL), F32), pltpu.VMEM((NBASIS, C, JL), F32)),
+    )(disco_dlat, disco_dlon, disco_basis, disco_quad, x, up, down, wt)
     after, normed = call(
-        conv_kernel,
-        "conv",
+        seam_kernel,
+        "seam", 12,
         (shape((C * TL, JL), F32), shape((C * TL, JL))),
-        in_specs=[smem] * 4 + [vmem] * 7,
-        scratch=(
-            pltpu.VMEM((60, C, JL), F32),
-            pltpu.VMEM((NBASIS, C, JL), F32),
-            pltpu.VMEM((C * TL, JL), F32),
-        ),
-    )(disco_dlat, disco_dlon, disco_basis, disco_quad, x, up, down, west, east, wt, gain)
+        in_specs=[smem] * 5 + [vmem] * 5,
+        scratch=(pltpu.VMEM((C * TL, JL), F32),),
+    )(core, disco_dlat, disco_dlon, disco_basis, disco_quad, inner, far, near, wt, gain)
 
     portion = exchanged(normed.reshape(32, CB * TL, JL), CHAN)
-    fourier = call(fourier_kernel, "fourier", shape((2 * MM, C)))(portion, fwd_hi, fwd_lo, lanes)
+    fourier = call(fourier_kernel, "fourier", 16, shape((2 * MM, C)))(portion, fwd_hi, fwd_lo, lanes)
     gathered = exchanged(fourier.reshape(16, 2 * ORD, C), RING)
     whole = pl.BlockSpec((2 * MM, C), lambda m: (0, 0))
-    table = pl.BlockSpec((1, LL, NLAT), lambda m: (m, 0, 0))
+    table = pl.BlockSpec((4, STEP, LL, NLAT), lambda m: (0, m, 0, 0))
     synthesis = call(
         spectral_kernel,
-        "spectral",
+        "spectral", 54,
         shape((2 * MM, C)),
-        grid=(ORD,),
-        in_specs=[whole] + [table] * 4 + [pl.BlockSpec((LL, 128), lambda m: (0, 0))],
+        grid=(ORD // STEP,),
+        in_specs=[whole, table, pl.BlockSpec((LL, 128), lambda m: (0, 0))],
         out_specs=whole,
         scratch=(
             pltpu.VMEM((3, 2 * MM, 128), F32),
-            pltpu.VMEM((NLAT, 128), F32),
+            pltpu.VMEM((STEP, NLAT, 128), F32),
             pltpu.VMEM((3, 2 * MM, 128), F32),
         ),
-    )(gathered.reshape(2 * MM, C), *tables, own)
+    )(gathered.reshape(2 * MM, C), tables, own)
     returned = exchanged(synthesis.reshape(16, 2 * ORD, C), RING)
-    activated = call(inverse_kernel, "inverse", shape((32, CB * TL, JL)))(
+    activated = call(inverse_kernel, "inverse", 16, shape((32, CB * TL, JL)))(
         returned.reshape(2 * MM, C), inv_hi, inv_lo, lanes
     )
     mixed = exchanged(activated, CHAN)
     out = call(
-        mix_kernel, "mix", shape((C * TL, JL), F32), scratch=(pltpu.VMEM((C * TL, JL), F32),)
+        mix_kernel, "mix", 12, shape((C * TL, JL), F32), scratch=(pltpu.VMEM((C * TL, JL), F32),)
     )(mixed.reshape(C * TL, JL), after, mixt)
     return out.reshape(C, TL, JL)
 

time: 198 us -> 163 us (0.82)
  blocking collectives: 101 us -> 76.4 us
  Pallas kernels: 61.3 us -> 39.9 us
  starting transfers between devices: 18.5 us -> 30.8 us
  waiting for transfers between devices: 13.1 us -> 10 us
  local copies, waits for them, and re-layouts: 2.45 us -> 4.7 us
    all_to_all x3, blocking collectives: 101 us -> 76.4 us  [exchanged(): return lax.all_to_all(blocks, axes, split_axis=0, concat_axis=0, tiled=True)]
    pallas_call x9 -> x10, Pallas kernels: 61.3 us -> 39.9 us  [the longest x1 10.1 us: per_device(): call(spectral_kernel, 'spectral', 54, shape((2 * MM, C)), grid=(ORD // ST...]
    ppermute x2, starting transfers between devices: 9.07 us -> 20.9 us  [the longest x1 15.1 us: per_device(): near = lax.ppermute(near, LON, pairs(lon_count, 0))]
    unnamed x15 -> x33, local copies, waits for them, and re-layouts: 1.56 us -> 4.61 us
    ppermute x1, waiting for transfers between devices: 3.73 us -> 1.34 us  [per_device(): down = lax.ppermute(first, LAT, [(i + 1, i) for i in range(lat_count - 1)])]
  transfers between devices with their start and end apart: 5 -> 5, of which waited for: 3 -> 2; matrix products, arithmetic and copies ran while one was open for 0% -> 1% of each run, Pallas kernels for 6% -> 12%
where the time goes in v2:
time: 163 us
  blocking collectives  76.4 us (47%)
  Pallas kernels  39.9 us (24%)
  starting transfers between devices  30.8 us (19%)
  waiting for transfers between devices  10 us (6%)
  local copies, waits for them, and re-layouts  4.7 us (3%)
    all_to_all x3, blocking collectives, exchanged(): return lax.all_to_all(blocks, axes, split_axis=0, concat_axis=0, tiled=True)  76.4 us
    ppermute x1, starting transfers between devices, per_device(): near = lax.ppermute(near, LON, pairs(lon_count, 0))  15.1 us
    pallas_call x1, Pallas kernels, per_device(): call(spectral_kernel, 'spectral', 54, shape((2 * MM, C)), grid=(ORD // ST...  10.1 us
    pallas_call x1, Pallas kernels, per_device(): call(conv_kernel, 'conv', 24, shape((C * TL, JL), F32), in_specs=[smem] *...  9.74 us
    pallas_call x1, Pallas kernels, per_device(): call(legendre_kernel, 'legendre', 57, shape((4, ORD, LL, NLAT)), in_specs...  9.08 us
    all_to_all x1, waiting for transfers between devices, exchanged(): return lax.all_to_all(blocks, axes, split_axis=0, concat_axis=0, tiled=True)  8.66 us
    ppermute x1, starting transfers between devices, per_device(): far = lax.ppermute(far, LON, pairs(lon_count, 1))  5.8 us
    unnamed x33, local copies, waits for them, and re-layouts  4.61 us
  transfers between devices with their start and end apart: 5, of which 2 were waited for; matrix products, arithmetic and copies ran while one was open for 1% of the time, Pallas kernels for 12%

profile of v2, /device:TPU:1, one launch (start us, length us, event | category | flops | bytes accessed | tf_op | source)
XLA Modules:
  0.0 162.7 jit_solution(16700970748414714318)
XLA Ops:
  0.0 1.5 copy-done.1
  1.5 0.2 rows.1
  1.6 4.2 %collective-permute-start = (bf16[768,128]{1,0:T(8,128)(2,1)S(1)}, bf16[768,128]{1,0:T(8,128)(2,1)S(1)}, u32[]{:S(2)}, u32[]{:S(2)}) collective-permute-start(bf16[768,128]{1,0:T(8,128)(2,1)S(1)} %get-tuple-element.20), channel_id=1, source_target_pairs={{0,16},{16,32},{32,48},{48,64},{64,80},{80,96},{96,112},{112,128},... | collective-permute-start | bytes 589832 | tf_op jit(solution)/shard_map/ppermute | solution.py:419
  5.8 1.3 collective-permute-start.1
  7.2 0.1 copy.19
  7.3 0.1 pad.2.clone
  7.4 1.3 copy-done.4
  8.6 1.0 copy-done.9
  9.6 0.5 weights.1
  10.1 0.8 maximum_bitcast_fusion.filter_ref
  10.9 0.0 collective-permute-done.up_ref
  10.9 1.3 collective-permute-done.1.down_ref
  12.2 0.7 edges.1
  12.9 5.8 %collective-permute-start.2 = (bf16[32,384]{1,0:T(8,128)(2,1)S(1)}, bf16[32,384]{1,0:T(8,128)(2,1)S(1)}, u32[]{:S(2)}, u32[]{:S(2)}) collective-permute-start(bf16[32,384]{1,0:T(8,128)(2,1)S(1)} %get-tuple-element.28), channel_id=1, source_target_pairs={{1,2},{3,4},{5,6},{7,8},{9,10},{11,12},{13,14},{15,0},{2,1},{4,3},... | collective-permute-start | bytes 73736 | tf_op jit(solution)/shard_map/ppermute | solution.py:434
  18.7 15.1 %collective-permute-start.3 = (bf16[32,384]{1,0:T(8,128)(2,1)S(1)}, bf16[32,384]{1,0:T(8,128)(2,1)S(1)}, u32[]{:S(2)}, u32[]{:S(2)}) collective-permute-start(bf16[32,384]{1,0:T(8,128)(2,1)S(1)} %get-tuple-element.29), channel_id=1, source_target_pairs={{0,1},{2,3},{4,5},{6,7},{8,9},{10,11},{12,13},{14,15},{1,0},{3,2},... | collective-permute-start | bytes 73736 | tf_op jit(solution)/shard_map/ppermute | solution.py:435
  33.9 9.7 %conv.1.inner_ref = f32[3072,128]{1,0:T(8,128)S(1)} custom-call(s32[8,16]{1,0:T(8,128)S(1)} %copy-done.10, s32[8,16]{1,0:T(8,128)S(1)} %copy-done.11, s32[8,16]{1,0:T(8,128)S(1)} %copy-done.12, f32[8,16]{1,0:T(8,128)S(1)} %copy-done.13, f32[3072,128]{1,0:T(8,128)S(1)} %bitcast.15, bf16[768,128]{1,0:T(8,128)(2,1)S(1)} %collective-permute-done.up_ref, ...), custom_call_target="tpu_custom_call" | custom-call | tf_op jit(solution)/shard_map/conv/pallas_call | solution.py:446
  43.6 0.0 copy-start.3
  43.6 0.0 copy-start.7
  43.7 0.0 copy-start.8
  43.7 0.0 collective-permute-done.2.far_ref
  43.7 2.9 %seam.1 = (f32[3072,128]{1,0:T(8,128)S(1)}, bf16[3072,128]{1,0:T(8,128)(2,1)S(1)}) custom-call(s32[1]{0:T(128)} %bitcast.core_ref, s32[8,16]{1,0:T(8,128)S(1)} %copy-done.10, s32[8,16]{1,0:T(8,128)S(1)} %copy-done.11, s32[8,16]{1,0:T(8,128)S(1)} %copy-done.12, f32[8,16]{1,0:T(8,128)S(1)} %copy-done.13, f32[3072,128]{1,0:T(8,128)S(1)} %conv.1.inner_ref, ...), custom_call_target="tpu_custom_call" | custom-call | tf_op jit(solution)/shard_map/seam/pallas_call | solution.py:453
  46.6 21.4 %all_to_all.20.recv_ref = bf16[32,96,128]{2,1,0:T(8,128)(2,1)S(1)} all-to-all(bf16[32,96,128]{2,1,0:T(8,128)(2,1)S(1)} %bitcast.19), channel_id=1, replica_groups=mesh['zl'=8,'y'=4,'zh'=2,'x'=4,'core'=2] {'y','x','core'}, dimensions={0} | all-to-all | bytes 1572864 | tf_op jit(solution)/shard_map/all_to_all | solution.py:391
  68.0 2.3 %fourier.1 = bf16[512,384]{1,0:T(8,128)(2,1)} custom-call(bf16[32,96,128]{2,1,0:T(8,128)(2,1)S(1)} %all_to_all.20.recv_ref, bf16[512,1024]{1,0:T(8,128)(2,1)S(1)} %copy-done.8, bf16[512,1024]{1,0:T(8,128)(2,1)S(1)} %copy-done.7, bf16[384,384]{1,0:T(8,128)(2,1)S(1)} %copy-done.3), custom_call_target="tpu_custom_call" | custom-call | tf_op jit(solution)/shard_map/fourier/pallas_call | solution.py:462
  70.3 4.4 %all-to-all-start.1 = ((bf16[16,32,384]{2,1,0:T(8,128)(2,1)}), bf16[16,32,384]{2,1,0:T(8,128)(2,1)S(1)}, u32[]{:S(2)}, u32[]{:S(2)}) async-start(bf16[16,32,384]{2,1,0:T(8,128)(2,1)} %bitcast.5), calls=%async_computation.1 | async-start | bytes 786432 | tf_op jit(solution)/shard_map/all_to_all | solution.py:391
  74.7 9.1 %legendre.1.table_ref = bf16[4,16,256,256]{3,2,1,0:T(8,128)(2,1)} custom-call(s32[1]{0:T(128)} %bitcast.7.place_ref, f32[2,256]{1,0:T(2,128)} %constant.48.clone.degree_ref, f32[256,128]{1,0:T(8,128)} %constant.49.clone.term_ref, f32[8,256]{1,0:T(8,128)} %constant.50.clone.lat_ref), custom_call_target="tpu_custom_call" | custom-call | tf_op jit(solution)/shard_map/legendre/pallas_call | solution.py:438
  83.8 8.7 %all-to-all-done.1 = bf16[16,32,384]{2,1,0:T(8,128)(2,1)S(1)} async-done(((bf16[16,32,384]{2,1,0:T(8,128)(2,1)}), bf16[16,32,384]{2,1,0:T(8,128)(2,1)S(1)}, u32[]{:S(2)}, u32[]{:S(2)}) %all-to-all-start.1) | async-done | bytes 393248 | tf_op jit(solution)/shard_map/all_to_all | solution.py:391
  92.5 0.7 copy-done.14
  93.2 10.1 %spectral.1 = bf16[512,384]{1,0:T(8,128)(2,1)} custom-call(bf16[512,384]{1,0:T(8,128)(2,1)} %bitcast.20, bf16[4,16,256,256]{3,2,1,0:T(8,128)(2,1)} %legendre.1.table_ref, f32[256,128]{1,0:T(8,128)} %maximum_bitcast_fusion.filter_ref), custom_call_target="tpu_custom_call" | custom-call | tf_op jit(solution)/shard_map/spectral/pallas_call | solution.py:466
  103.3 30.1 %all_to_all.21 = bf16[16,32,384]{2,1,0:T(8,128)(2,1)S(1)} all-to-all(bf16[16,32,384]{2,1,0:T(8,128)(2,1)} %bitcast.21), channel_id=1, replica_groups=mesh['zl'=8,'y'=4,'zh'=2,'x'=4,'core'=2] {'zh','zl'}, dimensions={0} | all-to-all | bytes 786432 | tf_op jit(solution)/shard_map/all_to_all | solution.py:391
  133.4 2.2 %inverse.1 = bf16[32,96,128]{2,1,0:T(8,128)(2,1)S(1)} custom-call(bf16[512,384]{1,0:T(8,128)(2,1)S(1)} %bitcast.17, bf16[512,1024]{1,0:T(8,128)(2,1)S(1)} %copy-done.6, bf16[512,1024]{1,0:T(8,128)(2,1)S(1)} %copy-done.5, bf16[384,384]{1,0:T(8,128)(2,1)S(1)} %copy-done.3), custom_call_target="tpu_custom_call" | custom-call | tf_op jit(solution)/shard_map/inverse/pallas_call | solution.py:480
  135.7 24.9 %all_to_all.22 = bf16[32,96,128]{2,1,0:T(8,128)(2,1)S(1)} all-to-all(bf16[32,96,128]{2,1,0:T(8,128)(2,1)S(1)} %inverse.1), channel_id=1, replica_groups=mesh['zl'=8,'y'=4,'zh'=2,'x'=4,'core'=2] {'y','x','core'}, dimensions={0} | all-to-all | bytes 1572864 | tf_op jit(solution)/shard_map/all_to_all | solution.py:391
  160.5 2.2 %mix.1 = f32[3072,128]{1,0:T(8,128)} custom-call(bf16[3072,128]{1,0:T(8,128)(2,1)S(1)} %bitcast.16, f32[3072,128]{1,0:T(8,128)S(1)} %get-tuple-element.33.after_ref, bf16[384,384]{1,0:T(8,128)(2,1)S(1)} %get-tuple-element.34.mixt_ref), custom_call_target="tpu_custom_call" | custom-call | tf_op jit(solution)/shard_map/mix/pallas_call | solution.py:484
  (29 shorter events, 0.1 us)
Async XLA Ops:
  0.0 7.1 %copy-start = (f32[384,256]{1,0:T(8,128)S(1)}, f32[384,256]{1,0:T(8,128)}, u32[]{:S(2)}) copy-start(f32[384,256]{1,0:T(8,128)} %param.24) | copy-start | bytes 1179652
  0.0 1.5 copy-start.1
  1.5 5.7 %copy-start.15 = (f32[384]{0:T(512)S(1)}, f32[384]{0:T(512)}, u32[]{:S(2)}) copy-start(f32[384]{0:T(512)} %param.23) | copy-start | bytes 4612
  1.5 10.8 %copy-start.2 = (f32[384,8,128]{2,1,0:T(8,128)S(1)}, f32[384,8,128]{2,1,0:T(8,128)}, u32[]{:S(2)}) copy-start(f32[384,8,128]{2,1,0:T(8,128)} %param.17) | copy-start | bytes 4718596
  1.6 9.2 %collective-permute-start = (bf16[768,128]{1,0:T(8,128)(2,1)S(1)}, bf16[768,128]{1,0:T(8,128)(2,1)S(1)}, u32[]{:S(2)}, u32[]{:S(2)}) collective-permute-start(bf16[768,128]{1,0:T(8,128)(2,1)S(1)} %get-tuple-element.20), channel_id=1, source_target_pairs={{0,16},{16,32},{32,48},{48,64},{64,80},{80,96},{96,112},{112,128},... | collective-permute-start | bytes 589832 | tf_op jit(solution)/shard_map/ppermute | solution.py:419
  5.8 6.4 %collective-permute-start.1 = (bf16[768,128]{1,0:T(8,128)(2,1)S(1)}, bf16[768,128]{1,0:T(8,128)(2,1)S(1)}, u32[]{:S(2)}, u32[]{:S(2)}) collective-permute-start(bf16[768,128]{1,0:T(8,128)(2,1)S(1)} %get-tuple-element.21), channel_id=1, source_target_pairs={{16,0},{32,16},{48,32},{64,48},{80,64},{96,80},{112,96},{128,112},... | collective-permute-start | bytes 589832 | tf_op jit(solution)/shard_map/ppermute | solution.py:420
  7.4 1.3 copy-start.4
  8.6 1.0 copy-start.9
  9.6 24.2 %copy-start.10 = (s32[8,16]{1,0:T(8,128)S(1)}, s32[8,16]{1,0:T(8,128)}, u32[]{:S(2)}) copy-start(s32[8,16]{1,0:T(8,128)} %dlat_ref.3) | copy-start | bytes 1540
  9.6 24.3 %copy-start.11 = (s32[8,16]{1,0:T(8,128)S(1)}, s32[8,16]{1,0:T(8,128)}, u32[]{:S(2)}) copy-start(s32[8,16]{1,0:T(8,128)} %dlon_ref.3) | copy-start | bytes 1540
  9.6 24.3 %copy-start.12 = (s32[8,16]{1,0:T(8,128)S(1)}, s32[8,16]{1,0:T(8,128)}, u32[]{:S(2)}) copy-start(s32[8,16]{1,0:T(8,128)} %basis_ref.3) | copy-start | bytes 1540
  9.6 24.3 %copy-start.13 = (f32[8,16]{1,0:T(8,128)S(1)}, f32[8,16]{1,0:T(8,128)}, u32[]{:S(2)}) copy-start(f32[8,16]{1,0:T(8,128)} %quad_ref.3) | copy-start | bytes 1540
  12.9 30.8 %collective-permute-start.2 = (bf16[32,384]{1,0:T(8,128)(2,1)S(1)}, bf16[32,384]{1,0:T(8,128)(2,1)S(1)}, u32[]{:S(2)}, u32[]{:S(2)}) collective-permute-start(bf16[32,384]{1,0:T(8,128)(2,1)S(1)} %get-tuple-element.28), channel_id=1, source_target_pairs={{1,2},{3,4},{5,6},{7,8},{9,10},{11,12},{13,14},{15,0},{2,1},{4,3},... | collective-permute-start | bytes 73736 | tf_op jit(solution)/shard_map/ppermute | solution.py:434
  18.7 25.0 %collective-permute-start.3 = (bf16[32,384]{1,0:T(8,128)(2,1)S(1)}, bf16[32,384]{1,0:T(8,128)(2,1)S(1)}, u32[]{:S(2)}, u32[]{:S(2)}) collective-permute-start(bf16[32,384]{1,0:T(8,128)(2,1)S(1)} %get-tuple-element.29), channel_id=1, source_target_pairs={{0,1},{2,3},{4,5},{6,7},{8,9},{10,11},{12,13},{14,15},{1,0},{3,2},... | collective-permute-start | bytes 73736 | tf_op jit(solution)/shard_map/ppermute | solution.py:435
  43.6 24.4 %copy-start.3 = (bf16[384,384]{1,0:T(8,128)(2,1)S(1)}, bf16[384,384]{1,0:T(8,128)(2,1)}, u32[]{:S(2)}) copy-start(bf16[384,384]{1,0:T(8,128)(2,1)} %constant.53.clone.lane_ref) | copy-start | bytes 884740
  43.6 24.4 %copy-start.7 = (bf16[512,1024]{1,0:T(8,128)(2,1)S(1)}, bf16[512,1024]{1,0:T(8,128)(2,1)}, u32[]{:S(2)}) copy-start(bf16[512,1024]{1,0:T(8,128)(2,1)} %constant.52.clone.lo_ref) | copy-start | bytes 3145732
  43.7 24.4 %copy-start.8 = (bf16[512,1024]{1,0:T(8,128)(2,1)S(1)}, bf16[512,1024]{1,0:T(8,128)(2,1)}, u32[]{:S(2)}) copy-start(bf16[512,1024]{1,0:T(8,128)(2,1)} %constant.51.clone.hi_ref) | copy-start | bytes 3145732
  70.3 22.1 %all-to-all-start.1 = ((bf16[16,32,384]{2,1,0:T(8,128)(2,1)}), bf16[16,32,384]{2,1,0:T(8,128)(2,1)S(1)}, u32[]{:S(2)}, u32[]{:S(2)}) async-start(bf16[16,32,384]{2,1,0:T(8,128)(2,1)} %bitcast.5), calls=%async_computation.1 | async-start | bytes 786432 | tf_op jit(solution)/shard_map/all_to_all | solution.py:391
  92.5 0.7 copy-start.14
  93.2 40.2 %copy-start.5 = (bf16[512,1024]{1,0:T(8,128)(2,1)S(1)}, bf16[512,1024]{1,0:T(8,128)(2,1)}, u32[]{:S(2)}) copy-start(bf16[512,1024]{1,0:T(8,128)(2,1)} %constant.55.clone.lo_ref) | copy-start | bytes 3145732
  93.2 40.2 %copy-start.6 = (bf16[512,1024]{1,0:T(8,128)(2,1)S(1)}, bf16[512,1024]{1,0:T(8,128)(2,1)}, u32[]{:S(2)}) copy-start(bf16[512,1024]{1,0:T(8,128)(2,1)} %constant.54.clone.hi_ref) | copy-start | bytes 3145732

commit v3 on v2

--- a/solution.py
+++ b/solution.py
@@ -187,8 +187,8 @@
         table = jnp.concatenate(
             [left_ref[pl.ds(m, LL, stride=ORD), :], right_ref[pl.ds(m, LL, stride=ORD), :]], axis=1
         )
-        table_ref[0, m], table_ref[1, m] = two_parts(table * quad)
-        table_ref[2, m], table_ref[3, m] = two_parts(table.T)
+        table_ref[0, m] = (table * quad).astype(BF16)
+        table_ref[1, m] = table.T.astype(BF16)
 
 
 def conv_kernel(
@@ -344,10 +344,10 @@
     filtered = []
     for i in range(STEP):
         fields = rows_ref[i].astype(BF16)
-        spectra = dot(table_ref[0, i], fields) + dot(table_ref[1, i], fields)
+        spectra = dot(table_ref[0, i], fields)
         filtered.append((spectra * filter_ref[...]).astype(BF16))
     for i in range(STEP):
-        rows_ref[i] = dot(table_ref[2, i], filtered[i]) + dot(table_ref[3, i], filtered[i])
+        rows_ref[i] = dot(table_ref[1, i], filtered[i])
     for i in range(STEP):
         found = [None] * 6
         for yt in range(32):
@@ -438,10 +438,11 @@
     tables = call(
         legendre_kernel,
         "legendre", 57,
-        shape((4, ORD, LL, NLAT)),
+        shape((2, ORD, LL, NLAT)),
         in_specs=[smem, smem, vmem, vmem],
         scratch=(pltpu.VMEM((LL * ORD, 128), F32), pltpu.VMEM((LL * ORD, 128), F32)),
     )(place, degree_terms(), order_terms(), latitude_rows())
+    tables = pltpu.with_memory_space_constraint(tables, pltpu.HBM)
 
     inner = call(
         conv_kernel,
@@ -462,10 +463,10 @@
     fourier = call(fourier_kernel, "fourier", 16, shape((2 * MM, C)))(portion, fwd_hi, fwd_lo, lanes)
     gathered = exchanged(fourier.reshape(16, 2 * ORD, C), RING)
     whole = pl.BlockSpec((2 * MM, C), lambda m: (0, 0))
-    table = pl.BlockSpec((4, STEP, LL, NLAT), lambda m: (0, m, 0, 0))
+    table = pl.BlockSpec((2, STEP, LL, NLAT), lambda m: (0, m, 0, 0))
     synthesis = call(
         spectral_kernel,
-        "spectral", 54,
+        "spectral", 14,
         shape((2 * MM, C)),
         grid=(ORD // STEP,),
         in_specs=[whole, table, pl.BlockSpec((LL, 128), lambda m: (0, 0))],

time: 163 us -> 160 us (0.982)
  Pallas kernels: 39.9 us -> 36.3 us
  waiting for transfers between devices: 10 us -> 12.2 us
    pallas_call x2, Pallas kernels: 19.2 us -> 15.6 us  [the longest x1 8.06 us: per_device(): call(spectral_kernel, 'spectral', 14, shape((2 * MM, C)), grid=(ORD // ST...]
    unnamed x33 -> x31, local copies, waits for them, and re-layouts: 4.61 us -> 3.86 us
  transfers between devices with their start and end apart: 5 -> 5, of which waited for: 2 -> 2; matrix products, arithmetic and copies ran while one was open for 1% -> 0% of each run, Pallas kernels for 12% -> 11%
where the time goes in v3:
time: 160 us
  blocking collectives  76.3 us (48%)
  Pallas kernels  36.3 us (23%)
  starting transfers between devices  30.8 us (19%)
  waiting for transfers between devices  12.2 us (8%)
  local copies, waits for them, and re-layouts  3.95 us (2%)
    all_to_all x3, blocking collectives, exchanged(): return lax.all_to_all(blocks, axes, split_axis=0, concat_axis=0, tiled=True)  76.3 us
    ppermute x1, starting transfers between devices, per_device(): near = lax.ppermute(near, LON, pairs(lon_count, 0))  15.1 us
    all_to_all x1, waiting for transfers between devices, exchanged(): return lax.all_to_all(blocks, axes, split_axis=0, concat_axis=0, tiled=True)  10.2 us
    pallas_call x1, Pallas kernels, per_device(): call(conv_kernel, 'conv', 24, shape((C * TL, JL), F32), in_specs=[smem] *...  9.74 us
    pallas_call x1, Pallas kernels, per_device(): call(spectral_kernel, 'spectral', 14, shape((2 * MM, C)), grid=(ORD // ST...  8.06 us
    pallas_call x1, Pallas kernels, per_device(): call(legendre_kernel, 'legendre', 57, shape((2, ORD, LL, NLAT)), in_specs...  7.58 us
    ppermute x1, starting transfers between devices, per_device(): far = lax.ppermute(far, LON, pairs(lon_count, 1))  5.8 us
    all_to_all x1, starting transfers between devices, exchanged(): return lax.all_to_all(blocks, axes, split_axis=0, concat_axis=0, tiled=True)  4.38 us
  transfers between devices with their start and end apart: 5, of which 2 were waited for; matrix products, arithmetic and copies ran while one was open for 0% of the time, Pallas kernels for 11%

profile of v3, /device:TPU:1, one launch (start us, length us, event | category | flops | bytes accessed | tf_op | source)
XLA Modules:
  0.0 159.9 jit_solution(16769204102937318610)
XLA Ops:
  0.0 1.5 copy-done.1
  1.5 0.2 rows.1
  1.6 4.2 %collective-permute-start = (bf16[768,128]{1,0:T(8,128)(2,1)S(1)}, bf16[768,128]{1,0:T(8,128)(2,1)S(1)}, u32[]{:S(2)}, u32[]{:S(2)}) collective-permute-start(bf16[768,128]{1,0:T(8,128)(2,1)S(1)} %get-tuple-element.20), channel_id=1, source_target_pairs={{0,16},{16,32},{32,48},{48,64},{64,80},{80,96},{96,112},{112,128},... | collective-permute-start | bytes 589832 | tf_op jit(solution)/shard_map/ppermute | solution.py:419
  5.8 1.3 collective-permute-start.1
  7.2 0.1 copy.19
  7.3 0.1 pad.2.clone
  7.4 1.3 copy-done.4
  8.6 1.0 copy-done.9
  9.6 0.5 weights.1
  10.1 0.1 maximum_bitcast_fusion.filter_ref
  10.2 0.0 collective-permute-done.up_ref
  10.2 2.0 %collective-permute-done.1.down_ref = bf16[768,128]{1,0:T(8,128)(2,1)S(1)} collective-permute-done((bf16[768,128]{1,0:T(8,128)(2,1)S(1)}, bf16[768,128]{1,0:T(8,128)(2,1)S(1)}, u32[]{:S(2)}, u32[]{:S(2)}) %collective-permute-start.1) | collective-permute-done | bytes 196640 | tf_op jit(solution)/shard_map/ppermute | solution.py:420
  12.2 0.7 edges.1
  12.9 5.8 %collective-permute-start.2 = (bf16[32,384]{1,0:T(8,128)(2,1)S(1)}, bf16[32,384]{1,0:T(8,128)(2,1)S(1)}, u32[]{:S(2)}, u32[]{:S(2)}) collective-permute-start(bf16[32,384]{1,0:T(8,128)(2,1)S(1)} %get-tuple-element.28), channel_id=1, source_target_pairs={{1,2},{3,4},{5,6},{7,8},{9,10},{11,12},{13,14},{15,0},{2,1},{4,3},... | collective-permute-start | bytes 73736 | tf_op jit(solution)/shard_map/ppermute | solution.py:434
  18.7 15.1 %collective-permute-start.3 = (bf16[32,384]{1,0:T(8,128)(2,1)S(1)}, bf16[32,384]{1,0:T(8,128)(2,1)S(1)}, u32[]{:S(2)}, u32[]{:S(2)}) collective-permute-start(bf16[32,384]{1,0:T(8,128)(2,1)S(1)} %get-tuple-element.29), channel_id=1, source_target_pairs={{0,1},{2,3},{4,5},{6,7},{8,9},{10,11},{12,13},{14,15},{1,0},{3,2},... | collective-permute-start | bytes 73736 | tf_op jit(solution)/shard_map/ppermute | solution.py:435
  33.9 9.7 %conv.1.inner_ref = f32[3072,128]{1,0:T(8,128)S(1)} custom-call(s32[8,16]{1,0:T(8,128)S(1)} %copy-done.10, s32[8,16]{1,0:T(8,128)S(1)} %copy-done.11, s32[8,16]{1,0:T(8,128)S(1)} %copy-done.12, f32[8,16]{1,0:T(8,128)S(1)} %copy-done.13, f32[3072,128]{1,0:T(8,128)S(1)} %bitcast.15, bf16[768,128]{1,0:T(8,128)(2,1)S(1)} %collective-permute-done.up_ref, ...), custom_call_target="tpu_custom_call" | custom-call | tf_op jit(solution)/shard_map/conv/pallas_call | solution.py:447
  43.6 0.0 copy-start.3
  43.6 0.0 copy-start.7
  43.7 0.0 copy-start.8
  43.7 0.0 collective-permute-done.2.far_ref
  43.7 0.0 collective-permute-done.3.near_ref
  43.7 2.9 %seam.1 = (f32[3072,128]{1,0:T(8,128)S(1)}, bf16[3072,128]{1,0:T(8,128)(2,1)S(1)}) custom-call(s32[1]{0:T(128)} %bitcast.core_ref, s32[8,16]{1,0:T(8,128)S(1)} %copy-done.10, s32[8,16]{1,0:T(8,128)S(1)} %copy-done.11, s32[8,16]{1,0:T(8,128)S(1)} %copy-done.12, f32[8,16]{1,0:T(8,128)S(1)} %copy-done.13, f32[3072,128]{1,0:T(8,128)S(1)} %conv.1.inner_ref, ...), custom_call_target="tpu_custom_call" | custom-call | tf_op jit(solution)/shard_map/seam/pallas_call | solution.py:454
  46.6 21.4 %all_to_all.20.recv_ref = bf16[32,96,128]{2,1,0:T(8,128)(2,1)S(1)} all-to-all(bf16[32,96,128]{2,1,0:T(8,128)(2,1)S(1)} %bitcast.21), channel_id=1, replica_groups=mesh['zl'=8,'y'=4,'zh'=2,'x'=4,'core'=2] {'y','x','core'}, dimensions={0} | all-to-all | bytes 1572864 | tf_op jit(solution)/shard_map/all_to_all | solution.py:391
  68.0 2.3 %fourier.1 = bf16[512,384]{1,0:T(8,128)(2,1)} custom-call(bf16[32,96,128]{2,1,0:T(8,128)(2,1)S(1)} %all_to_all.20.recv_ref, bf16[512,1024]{1,0:T(8,128)(2,1)S(1)} %copy-done.8, bf16[512,1024]{1,0:T(8,128)(2,1)S(1)} %copy-done.7, bf16[384,384]{1,0:T(8,128)(2,1)S(1)} %copy-done.3), custom_call_target="tpu_custom_call" | custom-call | tf_op jit(solution)/shard_map/fourier/pallas_call | solution.py:463
  70.3 4.4 %all-to-all-start.1 = ((bf16[16,32,384]{2,1,0:T(8,128)(2,1)}), bf16[16,32,384]{2,1,0:T(8,128)(2,1)S(1)}, u32[]{:S(2)}, u32[]{:S(2)}) async-start(bf16[16,32,384]{2,1,0:T(8,128)(2,1)} %bitcast.5), calls=%async_computation.1 | async-start | bytes 786432 | tf_op jit(solution)/shard_map/all_to_all | solution.py:391
  74.7 7.6 %legendre.1.table_ref = bf16[2,16,256,256]{3,2,1,0:T(8,128)(2,1)} custom-call(s32[1]{0:T(128)} %bitcast.7.place_ref, f32[2,256]{1,0:T(2,128)} %constant.48.clone.degree_ref, f32[256,128]{1,0:T(8,128)} %constant.49.clone.term_ref, f32[8,256]{1,0:T(8,128)} %constant.50.clone.lat_ref), custom_call_target="tpu_custom_call" | custom-call | tf_op jit(solution)/shard_map/legendre/pallas_call | solution.py:438
  82.3 10.2 %all-to-all-done.1 = bf16[16,32,384]{2,1,0:T(8,128)(2,1)S(1)} async-done(((bf16[16,32,384]{2,1,0:T(8,128)(2,1)}), bf16[16,32,384]{2,1,0:T(8,128)(2,1)S(1)}, u32[]{:S(2)}, u32[]{:S(2)}) %all-to-all-start.1) | async-done | bytes 393248 | tf_op jit(solution)/shard_map/all_to_all | solution.py:391
  92.5 8.1 %spectral.1 = bf16[512,384]{1,0:T(8,128)(2,1)S(1)} custom-call(bf16[512,384]{1,0:T(8,128)(2,1)S(1)} %bitcast.17, bf16[2,16,256,256]{3,2,1,0:T(8,128)(2,1)} %legendre.1.table_ref, f32[256,128]{1,0:T(8,128)S(1)} %maximum_bitcast_fusion.filter_ref), custom_call_target="tpu_custom_call" | custom-call | tf_op jit(solution)/shard_map/spectral/pallas_call | solution.py:467
  100.5 30.0 %all_to_all.21 = bf16[16,32,384]{2,1,0:T(8,128)(2,1)S(1)} all-to-all(bf16[16,32,384]{2,1,0:T(8,128)(2,1)S(1)} %bitcast.19), channel_id=1, replica_groups=mesh['zl'=8,'y'=4,'zh'=2,'x'=4,'core'=2] {'zh','zl'}, dimensions={0} | all-to-all | bytes 786432 | tf_op jit(solution)/shard_map/all_to_all | solution.py:391
  130.5 2.2 %inverse.1 = bf16[32,96,128]{2,1,0:T(8,128)(2,1)S(1)} custom-call(bf16[512,384]{1,0:T(8,128)(2,1)S(1)} %bitcast.18, bf16[512,1024]{1,0:T(8,128)(2,1)S(1)} %copy-done.6, bf16[512,1024]{1,0:T(8,128)(2,1)S(1)} %copy-done.5, bf16[384,384]{1,0:T(8,128)(2,1)S(1)} %copy-done.3), custom_call_target="tpu_custom_call" | custom-call | tf_op jit(solution)/shard_map/inverse/pallas_call | solution.py:481
  132.8 24.9 %all_to_all.22 = bf16[32,96,128]{2,1,0:T(8,128)(2,1)S(1)} all-to-all(bf16[32,96,128]{2,1,0:T(8,128)(2,1)S(1)} %inverse.1), channel_id=1, replica_groups=mesh['zl'=8,'y'=4,'zh'=2,'x'=4,'core'=2] {'y','x','core'}, dimensions={0} | all-to-all | bytes 1572864 | tf_op jit(solution)/shard_map/all_to_all | solution.py:391
  157.7 2.2 %mix.1 = f32[3072,128]{1,0:T(8,128)} custom-call(bf16[3072,128]{1,0:T(8,128)(2,1)S(1)} %bitcast.16, f32[3072,128]{1,0:T(8,128)S(1)} %get-tuple-element.33.after_ref, bf16[384,384]{1,0:T(8,128)(2,1)S(1)} %get-tuple-element.34.mixt_ref), custom_call_target="tpu_custom_call" | custom-call | tf_op jit(solution)/shard_map/mix/pallas_call | solution.py:485
  (27 shorter events, 0.1 us)
Async XLA Ops:
  0.0 7.1 %copy-start = (f32[384,256]{1,0:T(8,128)S(1)}, f32[384,256]{1,0:T(8,128)}, u32[]{:S(2)}) copy-start(f32[384,256]{1,0:T(8,128)} %param.24) | copy-start | bytes 1179652
  0.0 1.5 copy-start.1
  1.5 5.7 %copy-start.14 = (f32[384]{0:T(512)S(1)}, f32[384]{0:T(512)}, u32[]{:S(2)}) copy-start(f32[384]{0:T(512)} %param.23) | copy-start | bytes 4612
  1.5 10.8 %copy-start.2 = (f32[384,8,128]{2,1,0:T(8,128)S(1)}, f32[384,8,128]{2,1,0:T(8,128)}, u32[]{:S(2)}) copy-start(f32[384,8,128]{2,1,0:T(8,128)} %param.17) | copy-start | bytes 4718596
  1.6 8.6 %collective-permute-start = (bf16[768,128]{1,0:T(8,128)(2,1)S(1)}, bf16[768,128]{1,0:T(8,128)(2,1)S(1)}, u32[]{:S(2)}, u32[]{:S(2)}) collective-permute-start(bf16[768,128]{1,0:T(8,128)(2,1)S(1)} %get-tuple-element.20), channel_id=1, source_target_pairs={{0,16},{16,32},{32,48},{48,64},{64,80},{80,96},{96,112},{112,128},... | collective-permute-start | bytes 589832 | tf_op jit(solution)/shard_map/ppermute | solution.py:419
  5.8 6.4 %collective-permute-start.1 = (bf16[768,128]{1,0:T(8,128)(2,1)S(1)}, bf16[768,128]{1,0:T(8,128)(2,1)S(1)}, u32[]{:S(2)}, u32[]{:S(2)}) collective-permute-start(bf16[768,128]{1,0:T(8,128)(2,1)S(1)} %get-tuple-element.21), channel_id=1, source_target_pairs={{16,0},{32,16},{48,32},{64,48},{80,64},{96,80},{112,96},{128,112},... | collective-permute-start | bytes 589832 | tf_op jit(solution)/shard_map/ppermute | solution.py:420
  7.4 1.3 copy-start.4
  8.6 1.0 copy-start.9
  9.6 24.2 %copy-start.10 = (s32[8,16]{1,0:T(8,128)S(1)}, s32[8,16]{1,0:T(8,128)}, u32[]{:S(2)}) copy-start(s32[8,16]{1,0:T(8,128)} %dlat_ref.3) | copy-start | bytes 1540
  9.6 24.3 %copy-start.11 = (s32[8,16]{1,0:T(8,128)S(1)}, s32[8,16]{1,0:T(8,128)}, u32[]{:S(2)}) copy-start(s32[8,16]{1,0:T(8,128)} %dlon_ref.3) | copy-start | bytes 1540
  9.6 24.3 %copy-start.12 = (s32[8,16]{1,0:T(8,128)S(1)}, s32[8,16]{1,0:T(8,128)}, u32[]{:S(2)}) copy-start(s32[8,16]{1,0:T(8,128)} %basis_ref.3) | copy-start | bytes 1540
  9.6 24.3 %copy-start.13 = (f32[8,16]{1,0:T(8,128)S(1)}, f32[8,16]{1,0:T(8,128)}, u32[]{:S(2)}) copy-start(f32[8,16]{1,0:T(8,128)} %quad_ref.3) | copy-start | bytes 1540
  12.9 30.8 %collective-permute-start.2 = (bf16[32,384]{1,0:T(8,128)(2,1)S(1)}, bf16[32,384]{1,0:T(8,128)(2,1)S(1)}, u32[]{:S(2)}, u32[]{:S(2)}) collective-permute-start(bf16[32,384]{1,0:T(8,128)(2,1)S(1)} %get-tuple-element.28), channel_id=1, source_target_pairs={{1,2},{3,4},{5,6},{7,8},{9,10},{11,12},{13,14},{15,0},{2,1},{4,3},... | collective-permute-start | bytes 73736 | tf_op jit(solution)/shard_map/ppermute | solution.py:434
  18.7 25.0 %collective-permute-start.3 = (bf16[32,384]{1,0:T(8,128)(2,1)S(1)}, bf16[32,384]{1,0:T(8,128)(2,1)S(1)}, u32[]{:S(2)}, u32[]{:S(2)}) collective-permute-start(bf16[32,384]{1,0:T(8,128)(2,1)S(1)} %get-tuple-element.29), channel_id=1, source_target_pairs={{0,1},{2,3},{4,5},{6,7},{8,9},{10,11},{12,13},{14,15},{1,0},{3,2},... | collective-permute-start | bytes 73736 | tf_op jit(solution)/shard_map/ppermute | solution.py:435
  43.6 24.4 %copy-start.3 = (bf16[384,384]{1,0:T(8,128)(2,1)S(1)}, bf16[384,384]{1,0:T(8,128)(2,1)}, u32[]{:S(2)}) copy-start(bf16[384,384]{1,0:T(8,128)(2,1)} %constant.53.clone.lane_ref) | copy-start | bytes 884740
  43.6 24.4 %copy-start.7 = (bf16[512,1024]{1,0:T(8,128)(2,1)S(1)}, bf16[512,1024]{1,0:T(8,128)(2,1)}, u32[]{:S(2)}) copy-start(bf16[512,1024]{1,0:T(8,128)(2,1)} %constant.52.clone.lo_ref) | copy-start | bytes 3145732
  43.7 24.4 %copy-start.8 = (bf16[512,1024]{1,0:T(8,128)(2,1)S(1)}, bf16[512,1024]{1,0:T(8,128)(2,1)}, u32[]{:S(2)}) copy-start(bf16[512,1024]{1,0:T(8,128)(2,1)} %constant.51.clone.hi_ref) | copy-start | bytes 3145732
  70.3 22.1 %all-to-all-start.1 = ((bf16[16,32,384]{2,1,0:T(8,128)(2,1)}), bf16[16,32,384]{2,1,0:T(8,128)(2,1)S(1)}, u32[]{:S(2)}, u32[]{:S(2)}) async-start(bf16[16,32,384]{2,1,0:T(8,128)(2,1)} %bitcast.5), calls=%async_computation.1 | async-start | bytes 786432 | tf_op jit(solution)/shard_map/all_to_all | solution.py:391
  92.5 38.1 %copy-start.5 = (bf16[512,1024]{1,0:T(8,128)(2,1)S(1)}, bf16[512,1024]{1,0:T(8,128)(2,1)}, u32[]{:S(2)}) copy-start(bf16[512,1024]{1,0:T(8,128)(2,1)} %constant.55.clone.lo_ref) | copy-start | bytes 3145732
  92.5 38.1 %copy-start.6 = (bf16[512,1024]{1,0:T(8,128)(2,1)S(1)}, bf16[512,1024]{1,0:T(8,128)(2,1)}, u32[]{:S(2)}) copy-start(bf16[512,1024]{1,0:T(8,128)(2,1)} %constant.54.clone.hi_ref) | copy-start | bytes 3145732

commit v4 on v3

--- a/solution.py
+++ b/solution.py
@@ -60,12 +60,6 @@
     return high, (value - high.astype(F32)).astype(BF16)
 
 
-def split_constant(table):
-    high = table.astype(np.float32).astype(jnp.bfloat16)
-    low = (table - high.astype(np.float64)).astype(np.float32).astype(jnp.bfloat16)
-    return high, low
-
-
 def longitude_tables():
     order = np.arange(MM)
     lon = np.arange(NLON // 2)
@@ -75,7 +69,8 @@
     both = both.transpose(1, 0, 2, 3).reshape(2 * MM, NLON // 2)
     weight = np.where(order == 0, 1.0, 2.0).reshape(MM // ORD, 1, ORD)
     weight = np.broadcast_to(weight, (MM // ORD, 2, ORD)).reshape(2 * MM, 1)
-    return split_constant(both * (2.0 * math.pi / NLON)), split_constant(both * weight)
+    forward = both * (2.0 * math.pi / NLON)
+    return forward.astype(jnp.bfloat16), (both * weight).astype(jnp.bfloat16)
 
 
 def lane_order():
@@ -304,7 +299,7 @@
     normed_ref[...] = scaled_ref[...].astype(BF16)
 
 
-def fourier_kernel(recv_ref, hi_ref, lo_ref, lane_ref, out_ref):
+def fourier_kernel(recv_ref, lon_ref, lane_ref, out_ref):
     circles = jnp.concatenate(
         [
             jnp.concatenate([recv_ref[8 * y + s] for s in range(8)], axis=1)
@@ -312,8 +307,7 @@
         ],
         axis=0,
     )
-    dims = ((1,), (1,))
-    found = dot(hi_ref[...], circles, dims) + dot(lo_ref[...], circles, dims)
+    found = dot(lon_ref[...], circles, ((1,), (1,)))
     out_ref[...] = dot(found.astype(BF16), lane_ref[...]).astype(BF16)
 
 
@@ -327,20 +321,24 @@
         for j in range(3):
             in_ref[j] = recv_ref[:, 128 * j : 128 * (j + 1)].astype(F32)
 
-    lane = lax.broadcasted_iota(jnp.int32, (8, 128), 1)
+    block = lax.broadcasted_iota(jnp.int32, (8, 128), 1) >> 2
+    orders = []
     for i in range(STEP):
         parts = []
         for r in range(2):
             for j in range(3):
                 near = in_ref[j, pl.ds(r * ORD + first + i, 8, stride=32), :]
                 far = in_ref[j, pl.ds(256 + r * ORD + first + i, 8, stride=32), :]
-                parts.append(near - far if i % 2 else near + far)
-        for yt in range(32):
-            tile = None
-            for n in range(6):
-                moved = pltpu.roll(parts[n], (4 * n - 4 * yt) % 128, 1)
-                tile = moved if tile is None else jnp.where(lane >= 4 * n, moved, tile)
-            rows_ref[i, pl.ds(8 * yt, 8), :] = tile
+                part = near - far if i % 2 else near + far
+                parts.append(pltpu.roll(part, 12 * r + 4 * j, 1) if r + j else part)
+        orders.append(parts)
+    for yt in range(32):
+        place = (block - yt) & 31
+        for i in range(STEP):
+            tile = orders[i][0]
+            for n in range(1, 6):
+                tile = jnp.where(place >= n, orders[i][n], tile)
+            rows_ref[i, pl.ds(8 * yt, 8), :] = pltpu.roll(tile, 128 - 4 * yt, 1) if yt else tile
     filtered = []
     for i in range(STEP):
         fields = rows_ref[i].astype(BF16)
@@ -348,16 +346,21 @@
         filtered.append((spectra * filter_ref[...]).astype(BF16))
     for i in range(STEP):
         rows_ref[i] = dot(table_ref[1, i], filtered[i])
+    found = [[None] * 6 for i in range(STEP)]
+    for yt in range(32):
+        place = (block - yt) & 31
+        for i in range(STEP):
+            tile = rows_ref[i, pl.ds(8 * yt, 8), :]
+            if yt:
+                tile = pltpu.roll(tile, 4 * yt, 1)
+            for n in range(6):
+                found[i][n] = jnp.where(place == n, tile, found[i][n]) if yt else tile
     for i in range(STEP):
-        found = [None] * 6
-        for yt in range(32):
-            tile = rows_ref[i, pl.ds(8 * yt, 8), :]
-            for n in range(6):
-                moved = pltpu.roll(tile, (4 * yt - 4 * n) % 128, 1)
-                found[n] = moved if yt == 0 else jnp.where(lane >= 4 * yt, moved, found[n])
         for r in range(2):
             for j in range(3):
-                value = found[3 * r + j]
+                value = found[i][3 * r + j]
+                if r + j:
+                    value = pltpu.roll(value, 128 - 12 * r - 4 * j, 1)
                 back_ref[j, pl.ds(r * ORD + first + i, 8, stride=32), :] = value
                 back_ref[j, pl.ds(256 + r * ORD + first + i, 8, stride=32), :] = (
                     -value if i % 2 else value
@@ -369,11 +372,11 @@
             out_ref[:, 128 * j : 128 * (j + 1)] = back_ref[j].astype(BF16)
 
 
-def inverse_kernel(recv_ref, hi_ref, lo_ref, lane_ref, out_ref):
+def inverse_kernel(recv_ref, lon_ref, lane_ref, out_ref):
     turned = dot(lane_ref[...], recv_ref[...], ((1,), (1,))).astype(BF16)
     for s in range(8):
         lons = pl.ds(128 * s, 128)
-        wave = dot(turned, hi_ref[:, lons]) + dot(turned, lo_ref[:, lons])
+        wave = dot(turned, lon_ref[:, lons])
         act = jax.nn.gelu(wave, approximate=True).astype(BF16)
         for y in range(4):
             out_ref[8 * y + s] = act[96 * y : 96 * (y + 1)]
@@ -407,7 +410,7 @@
     spectral_filter,
     mix_weight,
 ):
-    (fwd_hi, fwd_lo), (inv_hi, inv_lo) = longitude_tables()
+    forward, backward = longitude_tables()
     lanes = lane_order()
     smem = pl.BlockSpec(memory_space=pltpu.SMEM)
     vmem = pl.BlockSpec(memory_space=pltpu.VMEM)
@@ -460,7 +463,7 @@
     )(core, disco_dlat, disco_dlon, disco_basis, disco_quad, inner, far, near, wt, gain)
 
     portion = exchanged(normed.reshape(32, CB * TL, JL), CHAN)
-    fourier = call(fourier_kernel, "fourier", 16, shape((2 * MM, C)))(portion, fwd_hi, fwd_lo, lanes)
+    fourier = call(fourier_kernel, "fourier", 16, shape((2 * MM, C)))(portion, forward, lanes)
     gathered = exchanged(fourier.reshape(16, 2 * ORD, C), RING)
     whole = pl.BlockSpec((2 * MM, C), lambda m: (0, 0))
     table = pl.BlockSpec((2, STEP, LL, NLAT), lambda m: (0, m, 0, 0))
@@ -479,7 +482,7 @@
     )(gathered.reshape(2 * MM, C), tables, own)
     returned = exchanged(synthesis.reshape(16, 2 * ORD, C), RING)
     activated = call(inverse_kernel, "inverse", 16, shape((32, CB * TL, JL)))(
-        returned.reshape(2 * MM, C), inv_hi, inv_lo, lanes
+        returned.reshape(2 * MM, C), backward, lanes
     )
     mixed = exchanged(activated, CHAN)
     out = call(

time: 160 us -> 157 us (0.981)
  Pallas kernels: 36.3 us -> 32.9 us
    pallas_call x1, Pallas kernels: 8.06 us -> 6.06 us  [per_device(): call(spectral_kernel, 'spectral', 14, shape((2 * MM, C)), grid=(ORD // ST...]
    unnamed x31 -> x27, local copies, waits for them, and re-layouts: 3.86 us -> 3.85 us
where the time goes in v4:
time: 157 us; the launch traced here: 156 us
  blocking collectives  76.2 us (49%)
  Pallas kernels  32.9 us (21%)
  starting transfers between devices  30.8 us (20%)
  waiting for transfers between devices  12.1 us (8%)
  local copies, waits for them, and re-layouts  3.94 us (3%)
    all_to_all x3, blocking collectives, exchanged(): return lax.all_to_all(blocks, axes, split_axis=0, concat_axis=0, tiled=True)  76.2 us
    ppermute x1, starting transfers between devices, per_device(): near = lax.ppermute(near, LON, pairs(lon_count, 0))  15.1 us
    all_to_all x1, waiting for transfers between devices, exchanged(): return lax.all_to_all(blocks, axes, split_axis=0, concat_axis=0, tiled=True)  10.2 us
    pallas_call x1, Pallas kernels, per_device(): call(conv_kernel, 'conv', 24, shape((C * TL, JL), F32), in_specs=[smem] *...  9.74 us
    pallas_call x1, Pallas kernels, per_device(): call(legendre_kernel, 'legendre', 57, shape((2, ORD, LL, NLAT)), in_specs...  7.57 us
    pallas_call x1, Pallas kernels, per_device(): call(spectral_kernel, 'spectral', 14, shape((2 * MM, C)), grid=(ORD // ST...  6.06 us
    ppermute x1, starting transfers between devices, per_device(): far = lax.ppermute(far, LON, pairs(lon_count, 1))  5.8 us
    all_to_all x1, starting transfers between devices, exchanged(): return lax.all_to_all(blocks, axes, split_axis=0, concat_axis=0, tiled=True)  4.39 us
  transfers between devices with their start and end apart: 5, of which 2 were waited for; matrix products, arithmetic and copies ran while one was open for 0% of the time, Pallas kernels for 11%

profile of v4, /device:TPU:1, one launch (start us, length us, event | category | flops | bytes accessed | tf_op | source)
XLA Modules:
  0.0 156.3 jit_solution(12418054003115163506)
XLA Ops:
  0.0 1.5 copy-done.1
  1.5 0.2 rows.1
  1.6 4.2 %collective-permute-start = (bf16[768,128]{1,0:T(8,128)(2,1)S(1)}, bf16[768,128]{1,0:T(8,128)(2,1)S(1)}, u32[]{:S(2)}, u32[]{:S(2)}) collective-permute-start(bf16[768,128]{1,0:T(8,128)(2,1)S(1)} %get-tuple-element.20), channel_id=1, source_target_pairs={{0,16},{16,32},{32,48},{48,64},{64,80},{80,96},{96,112},{112,128},... | collective-permute-start | bytes 589832 | tf_op jit(solution)/shard_map/ppermute | solution.py:422
  5.8 1.3 collective-permute-start.1
  7.1 0.0 copy-done.12
  7.2 0.1 copy.17
  7.3 0.1 pad.2.clone
  7.4 1.3 copy-done.4
  8.6 1.0 copy-done.7
  9.6 0.5 weights.1
  10.1 0.1 maximum_bitcast_fusion.filter_ref
  10.2 0.0 collective-permute-done.up_ref
  10.2 2.0 %collective-permute-done.1.down_ref = bf16[768,128]{1,0:T(8,128)(2,1)S(1)} collective-permute-done((bf16[768,128]{1,0:T(8,128)(2,1)S(1)}, bf16[768,128]{1,0:T(8,128)(2,1)S(1)}, u32[]{:S(2)}, u32[]{:S(2)}) %collective-permute-start.1) | collective-permute-done | bytes 196640 | tf_op jit(solution)/shard_map/ppermute | solution.py:423
  12.2 0.7 edges.1
  12.9 5.8 %collective-permute-start.2 = (bf16[32,384]{1,0:T(8,128)(2,1)S(1)}, bf16[32,384]{1,0:T(8,128)(2,1)S(1)}, u32[]{:S(2)}, u32[]{:S(2)}) collective-permute-start(bf16[32,384]{1,0:T(8,128)(2,1)S(1)} %get-tuple-element.28), channel_id=1, source_target_pairs={{1,2},{3,4},{5,6},{7,8},{9,10},{11,12},{13,14},{15,0},{2,1},{4,3},... | collective-permute-start | bytes 73736 | tf_op jit(solution)/shard_map/ppermute | solution.py:437
  18.7 15.1 %collective-permute-start.3 = (bf16[32,384]{1,0:T(8,128)(2,1)S(1)}, bf16[32,384]{1,0:T(8,128)(2,1)S(1)}, u32[]{:S(2)}, u32[]{:S(2)}) collective-permute-start(bf16[32,384]{1,0:T(8,128)(2,1)S(1)} %get-tuple-element.29), channel_id=1, source_target_pairs={{0,1},{2,3},{4,5},{6,7},{8,9},{10,11},{12,13},{14,15},{1,0},{3,2},... | collective-permute-start | bytes 73736 | tf_op jit(solution)/shard_map/ppermute | solution.py:438
  33.9 9.7 %conv.1.inner_ref = f32[3072,128]{1,0:T(8,128)S(1)} custom-call(s32[8,16]{1,0:T(8,128)S(1)} %copy-done.8, s32[8,16]{1,0:T(8,128)S(1)} %copy-done.9, s32[8,16]{1,0:T(8,128)S(1)} %copy-done.10, f32[8,16]{1,0:T(8,128)S(1)} %copy-done.11, f32[3072,128]{1,0:T(8,128)S(1)} %bitcast.15, bf16[768,128]{1,0:T(8,128)(2,1)S(1)} %collective-permute-done.up_ref, ...), custom_call_target="tpu_custom_call" | custom-call | tf_op jit(solution)/shard_map/conv/pallas_call | solution.py:450
  43.6 0.0 copy-start.3
  43.6 0.0 copy-start.6
  43.7 0.0 collective-permute-done.2.far_ref
  43.7 0.0 collective-permute-done.3.near_ref
  43.7 2.9 %seam.1 = (f32[3072,128]{1,0:T(8,128)S(1)}, bf16[3072,128]{1,0:T(8,128)(2,1)S(1)}) custom-call(s32[1]{0:T(128)} %bitcast.core_ref, s32[8,16]{1,0:T(8,128)S(1)} %copy-done.8, s32[8,16]{1,0:T(8,128)S(1)} %copy-done.9, s32[8,16]{1,0:T(8,128)S(1)} %copy-done.10, f32[8,16]{1,0:T(8,128)S(1)} %copy-done.11, f32[3072,128]{1,0:T(8,128)S(1)} %conv.1.inner_ref, ...), custom_call_target="tpu_custom_call" | custom-call | tf_op jit(solution)/shard_map/seam/pallas_call | solution.py:457
  46.6 21.4 %all_to_all.20.recv_ref = bf16[32,96,128]{2,1,0:T(8,128)(2,1)S(1)} all-to-all(bf16[32,96,128]{2,1,0:T(8,128)(2,1)S(1)} %bitcast.21), channel_id=1, replica_groups=mesh['zl'=8,'y'=4,'zh'=2,'x'=4,'core'=2] {'y','x','core'}, dimensions={0} | all-to-all | bytes 1572864 | tf_op jit(solution)/shard_map/all_to_all | solution.py:394
  68.0 1.7 %fourier.1 = bf16[512,384]{1,0:T(8,128)(2,1)} custom-call(bf16[32,96,128]{2,1,0:T(8,128)(2,1)S(1)} %all_to_all.20.recv_ref, bf16[512,1024]{1,0:T(8,128)(2,1)S(1)} %copy-done.6, bf16[384,384]{1,0:T(8,128)(2,1)S(1)} %copy-done.3), custom_call_target="tpu_custom_call" | custom-call | tf_op jit(solution)/shard_map/fourier/pallas_call | solution.py:466
  69.8 4.4 %all-to-all-start.1 = ((bf16[16,32,384]{2,1,0:T(8,128)(2,1)}), bf16[16,32,384]{2,1,0:T(8,128)(2,1)S(1)}, u32[]{:S(2)}, u32[]{:S(2)}) async-start(bf16[16,32,384]{2,1,0:T(8,128)(2,1)} %bitcast.5), calls=%async_computation.1 | async-start | bytes 786432 | tf_op jit(solution)/shard_map/all_to_all | solution.py:394
  74.2 7.6 %legendre.1.table_ref = bf16[2,16,256,256]{3,2,1,0:T(8,128)(2,1)} custom-call(s32[1]{0:T(128)} %bitcast.7.place_ref, f32[2,256]{1,0:T(2,128)} %constant.44.clone.degree_ref, f32[256,128]{1,0:T(8,128)} %constant.45.clone.term_ref, f32[8,256]{1,0:T(8,128)} %constant.46.clone.lat_ref), custom_call_target="tpu_custom_call" | custom-call | tf_op jit(solution)/shard_map/legendre/pallas_call | solution.py:441
  81.7 10.2 %all-to-all-done.1 = bf16[16,32,384]{2,1,0:T(8,128)(2,1)S(1)} async-done(((bf16[16,32,384]{2,1,0:T(8,128)(2,1)}), bf16[16,32,384]{2,1,0:T(8,128)(2,1)S(1)}, u32[]{:S(2)}, u32[]{:S(2)}) %all-to-all-start.1) | async-done | bytes 393248 | tf_op jit(solution)/shard_map/all_to_all | solution.py:394
  91.9 6.1 %spectral.1 = bf16[512,384]{1,0:T(8,128)(2,1)S(1)} custom-call(bf16[512,384]{1,0:T(8,128)(2,1)S(1)} %bitcast.17, bf16[2,16,256,256]{3,2,1,0:T(8,128)(2,1)} %legendre.1.table_ref, f32[256,128]{1,0:T(8,128)S(1)} %maximum_bitcast_fusion.filter_ref), custom_call_target="tpu_custom_call" | custom-call | tf_op jit(solution)/shard_map/spectral/pallas_call | solution.py:470
  97.9 29.8 %all_to_all.21 = bf16[16,32,384]{2,1,0:T(8,128)(2,1)S(1)} all-to-all(bf16[16,32,384]{2,1,0:T(8,128)(2,1)S(1)} %bitcast.18), channel_id=1, replica_groups=mesh['zl'=8,'y'=4,'zh'=2,'x'=4,'core'=2] {'zh','zl'}, dimensions={0} | all-to-all | bytes 786432 | tf_op jit(solution)/shard_map/all_to_all | solution.py:394
  127.8 1.4 inverse.1
  129.2 24.9 %all_to_all.22 = bf16[32,96,128]{2,1,0:T(8,128)(2,1)S(1)} all-to-all(bf16[32,96,128]{2,1,0:T(8,128)(2,1)S(1)} %inverse.1), channel_id=1, replica_groups=mesh['zl'=8,'y'=4,'zh'=2,'x'=4,'core'=2] {'y','x','core'}, dimensions={0} | all-to-all | bytes 1572864 | tf_op jit(solution)/shard_map/all_to_all | solution.py:394
  154.1 2.2 %mix.1 = f32[3072,128]{1,0:T(8,128)} custom-call(bf16[3072,128]{1,0:T(8,128)(2,1)S(1)} %bitcast.16, f32[3072,128]{1,0:T(8,128)S(1)} %get-tuple-element.33.after_ref, bf16[384,384]{1,0:T(8,128)(2,1)S(1)} %get-tuple-element.34.mixt_ref), custom_call_target="tpu_custom_call" | custom-call | tf_op jit(solution)/shard_map/mix/pallas_call | solution.py:488
  (23 shorter events, 0.1 us)
Async XLA Ops:
  0.0 7.1 %copy-start = (f32[384,256]{1,0:T(8,128)S(1)}, f32[384,256]{1,0:T(8,128)}, u32[]{:S(2)}) copy-start(f32[384,256]{1,0:T(8,128)} %param.22) | copy-start | bytes 1179652
  0.0 1.5 copy-start.1
  1.5 5.7 %copy-start.12 = (f32[384]{0:T(512)S(1)}, f32[384]{0:T(512)}, u32[]{:S(2)}) copy-start(f32[384]{0:T(512)} %param.21) | copy-start | bytes 4612
  1.5 10.8 %copy-start.2 = (f32[384,8,128]{2,1,0:T(8,128)S(1)}, f32[384,8,128]{2,1,0:T(8,128)}, u32[]{:S(2)}) copy-start(f32[384,8,128]{2,1,0:T(8,128)} %param.15) | copy-start | bytes 4718596
  1.6 8.6 %collective-permute-start = (bf16[768,128]{1,0:T(8,128)(2,1)S(1)}, bf16[768,128]{1,0:T(8,128)(2,1)S(1)}, u32[]{:S(2)}, u32[]{:S(2)}) collective-permute-start(bf16[768,128]{1,0:T(8,128)(2,1)S(1)} %get-tuple-element.20), channel_id=1, source_target_pairs={{0,16},{16,32},{32,48},{48,64},{64,80},{80,96},{96,112},{112,128},... | collective-permute-start | bytes 589832 | tf_op jit(solution)/shard_map/ppermute | solution.py:422
  5.8 6.4 %collective-permute-start.1 = (bf16[768,128]{1,0:T(8,128)(2,1)S(1)}, bf16[768,128]{1,0:T(8,128)(2,1)S(1)}, u32[]{:S(2)}, u32[]{:S(2)}) collective-permute-start(bf16[768,128]{1,0:T(8,128)(2,1)S(1)} %get-tuple-element.21), channel_id=1, source_target_pairs={{16,0},{32,16},{48,32},{64,48},{80,64},{96,80},{112,96},{128,112},... | collective-permute-start | bytes 589832 | tf_op jit(solution)/shard_map/ppermute | solution.py:423
  7.4 1.3 copy-start.4
  8.6 1.0 copy-start.7
  9.6 24.2 %copy-start.8 = (s32[8,16]{1,0:T(8,128)S(1)}, s32[8,16]{1,0:T(8,128)}, u32[]{:S(2)}) copy-start(s32[8,16]{1,0:T(8,128)} %dlat_ref.3) | copy-start | bytes 1540
  9.6 24.3 %copy-start.9 = (s32[8,16]{1,0:T(8,128)S(1)}, s32[8,16]{1,0:T(8,128)}, u32[]{:S(2)}) copy-start(s32[8,16]{1,0:T(8,128)} %dlon_ref.3) | copy-start | bytes 1540
  9.6 24.3 %copy-start.10 = (s32[8,16]{1,0:T(8,128)S(1)}, s32[8,16]{1,0:T(8,128)}, u32[]{:S(2)}) copy-start(s32[8,16]{1,0:T(8,128)} %basis_ref.3) | copy-start | bytes 1540
  9.6 24.3 %copy-start.11 = (f32[8,16]{1,0:T(8,128)S(1)}, f32[8,16]{1,0:T(8,128)}, u32[]{:S(2)}) copy-start(f32[8,16]{1,0:T(8,128)} %quad_ref.3) | copy-start | bytes 1540
  12.9 30.8 %collective-permute-start.2 = (bf16[32,384]{1,0:T(8,128)(2,1)S(1)}, bf16[32,384]{1,0:T(8,128)(2,1)S(1)}, u32[]{:S(2)}, u32[]{:S(2)}) collective-permute-start(bf16[32,384]{1,0:T(8,128)(2,1)S(1)} %get-tuple-element.28), channel_id=1, source_target_pairs={{1,2},{3,4},{5,6},{7,8},{9,10},{11,12},{13,14},{15,0},{2,1},{4,3},... | collective-permute-start | bytes 73736 | tf_op jit(solution)/shard_map/ppermute | solution.py:437
  18.7 25.0 %collective-permute-start.3 = (bf16[32,384]{1,0:T(8,128)(2,1)S(1)}, bf16[32,384]{1,0:T(8,128)(2,1)S(1)}, u32[]{:S(2)}, u32[]{:S(2)}) collective-permute-start(bf16[32,384]{1,0:T(8,128)(2,1)S(1)} %get-tuple-element.29), channel_id=1, source_target_pairs={{0,1},{2,3},{4,5},{6,7},{8,9},{10,11},{12,13},{14,15},{1,0},{3,2},... | collective-permute-start | bytes 73736 | tf_op jit(solution)/shard_map/ppermute | solution.py:438
  43.6 24.4 %copy-start.3 = (bf16[384,384]{1,0:T(8,128)(2,1)S(1)}, bf16[384,384]{1,0:T(8,128)(2,1)}, u32[]{:S(2)}) copy-start(bf16[384,384]{1,0:T(8,128)(2,1)} %constant.48.clone.lane_ref) | copy-start | bytes 884740
  43.6 24.4 %copy-start.6 = (bf16[512,1024]{1,0:T(8,128)(2,1)S(1)}, bf16[512,1024]{1,0:T(8,128)(2,1)}, u32[]{:S(2)}) copy-start(bf16[512,1024]{1,0:T(8,128)(2,1)} %constant.47.clone.lon_ref) | copy-start | bytes 3145732
  69.8 22.1 %all-to-all-start.1 = ((bf16[16,32,384]{2,1,0:T(8,128)(2,1)}), bf16[16,32,384]{2,1,0:T(8,128)(2,1)S(1)}, u32[]{:S(2)}, u32[]{:S(2)}) async-start(bf16[16,32,384]{2,1,0:T(8,128)(2,1)} %bitcast.5), calls=%async_computation.1 | async-start | bytes 786432 | tf_op jit(solution)/shard_map/all_to_all | solution.py:394
  91.9 35.9 %copy-start.5 = (bf16[512,1024]{1,0:T(8,128)(2,1)S(1)}, bf16[512,1024]{1,0:T(8,128)(2,1)}, u32[]{:S(2)}) copy-start(bf16[512,1024]{1,0:T(8,128)(2,1)} %constant.49.clone.lon_ref) | copy-start | bytes 3145732

commit v5 on v4

--- a/solution.py
+++ b/solution.py
@@ -23,7 +23,7 @@
 STEP = 4
 LAT = ("zl", "y")
 LON = ("zh", "x", "core")
-CHAN = ("y", "x", "core")
+CHAN = ("x", "y", "core")
 RING = ("zh", "zl")
 F32 = jnp.float32
 BF16 = jnp.bfloat16
@@ -299,10 +299,14 @@
     normed_ref[...] = scaled_ref[...].astype(BF16)
 
 
+def chan_block(y, s):
+    return s // 2 * 8 + y * 2 + s % 2
+
+
 def fourier_kernel(recv_ref, lon_ref, lane_ref, out_ref):
     circles = jnp.concatenate(
         [
-            jnp.concatenate([recv_ref[8 * y + s] for s in range(8)], axis=1)
+            jnp.concatenate([recv_ref[chan_block(y, s)] for s in range(8)], axis=1)
             for y in range(4)
         ],
         axis=0,
@@ -379,7 +383,7 @@
         wave = dot(turned, lon_ref[:, lons])
         act = jax.nn.gelu(wave, approximate=True).astype(BF16)
         for y in range(4):
-            out_ref[8 * y + s] = act[96 * y : 96 * (y + 1)]
+            out_ref[chan_block(y, s)] = act[96 * y : 96 * (y + 1)]
 
 
 def mix_kernel(act_ref, after_ref, mixt_ref, out_ref, wide_ref):

time: 157 us -> 156 us (level)
  blocking collectives: 76.2 us -> 74.1 us
  waiting for transfers between devices: 12.1 us -> 13.8 us
    all_to_all x3, blocking collectives: 76.2 us -> 74.1 us  [exchanged(): return lax.all_to_all(blocks, axes, split_axis=0, concat_axis=0, tiled=True)]
    all_to_all x1, waiting for transfers between devices: 10.2 us -> 11.8 us  [exchanged(): return lax.all_to_all(blocks, axes, split_axis=0, concat_axis=0, tiled=True)]
where the time goes in v5:
time: 156 us
  blocking collectives  74.1 us (47%)
  Pallas kernels  32.9 us (21%)
  starting transfers between devices  30.8 us (20%)
  waiting for transfers between devices  13.8 us (9%)
  local copies, waits for them, and re-layouts  3.94 us (3%)
    all_to_all x3, blocking collectives, exchanged(): return lax.all_to_all(blocks, axes, split_axis=0, concat_axis=0, tiled=True)  74.1 us
    ppermute x1, starting transfers between devices, per_device(): near = lax.ppermute(near, LON, pairs(lon_count, 0))  15.1 us
    all_to_all x1, waiting for transfers between devices, exchanged(): return lax.all_to_all(blocks, axes, split_axis=0, concat_axis=0, tiled=True)  11.8 us
    pallas_call x1, Pallas kernels, per_device(): call(conv_kernel, 'conv', 24, shape((C * TL, JL), F32), in_specs=[smem] *...  9.74 us
    pallas_call x1, Pallas kernels, per_device(): call(legendre_kernel, 'legendre', 57, shape((2, ORD, LL, NLAT)), in_specs...  7.57 us
    pallas_call x1, Pallas kernels, per_device(): call(spectral_kernel, 'spectral', 14, shape((2 * MM, C)), grid=(ORD // ST...  6.05 us
    ppermute x1, starting transfers between devices, per_device(): far = lax.ppermute(far, LON, pairs(lon_count, 1))  5.8 us
    all_to_all x1, starting transfers between devices, exchanged(): return lax.all_to_all(blocks, axes, split_axis=0, concat_axis=0, tiled=True)  4.39 us
  transfers between devices with their start and end apart: 5, of which 2 were waited for; matrix products, arithmetic and copies ran while one was open for 0% of the time, Pallas kernels for 11%

profile of v5, /device:TPU:1, one launch (start us, length us, event | category | flops | bytes accessed | tf_op | source)
XLA Modules:
  0.0 155.9 jit_solution(4039210806081482334)
XLA Ops:
  0.0 1.5 copy-done.1
  1.5 0.2 rows.1
  1.6 4.2 %collective-permute-start = (bf16[768,128]{1,0:T(8,128)(2,1)S(1)}, bf16[768,128]{1,0:T(8,128)(2,1)S(1)}, u32[]{:S(2)}, u32[]{:S(2)}) collective-permute-start(bf16[768,128]{1,0:T(8,128)(2,1)S(1)} %get-tuple-element.20), channel_id=1, source_target_pairs={{0,16},{16,32},{32,48},{48,64},{64,80},{80,96},{96,112},{112,128},... | collective-permute-start | bytes 589832 | tf_op jit(solution)/shard_map/ppermute | solution.py:426
  5.8 1.3 collective-permute-start.1
  7.1 0.0 copy-done
  7.2 0.1 copy.17
  7.3 0.1 pad.2.clone
  7.4 1.3 copy-done.4
  8.6 1.0 copy-done.7
  9.6 0.5 weights.1
  10.1 0.1 maximum_bitcast_fusion.filter_ref
  10.2 0.0 collective-permute-done.up_ref
  10.2 2.0 %collective-permute-done.1.down_ref = bf16[768,128]{1,0:T(8,128)(2,1)S(1)} collective-permute-done((bf16[768,128]{1,0:T(8,128)(2,1)S(1)}, bf16[768,128]{1,0:T(8,128)(2,1)S(1)}, u32[]{:S(2)}, u32[]{:S(2)}) %collective-permute-start.1) | collective-permute-done | bytes 196640 | tf_op jit(solution)/shard_map/ppermute | solution.py:427
  12.2 0.7 edges.1
  12.9 5.8 %collective-permute-start.2 = (bf16[32,384]{1,0:T(8,128)(2,1)S(1)}, bf16[32,384]{1,0:T(8,128)(2,1)S(1)}, u32[]{:S(2)}, u32[]{:S(2)}) collective-permute-start(bf16[32,384]{1,0:T(8,128)(2,1)S(1)} %get-tuple-element.28), channel_id=1, source_target_pairs={{1,2},{3,4},{5,6},{7,8},{9,10},{11,12},{13,14},{15,0},{2,1},{4,3},... | collective-permute-start | bytes 73736 | tf_op jit(solution)/shard_map/ppermute | solution.py:441
  18.7 15.1 %collective-permute-start.3 = (bf16[32,384]{1,0:T(8,128)(2,1)S(1)}, bf16[32,384]{1,0:T(8,128)(2,1)S(1)}, u32[]{:S(2)}, u32[]{:S(2)}) collective-permute-start(bf16[32,384]{1,0:T(8,128)(2,1)S(1)} %get-tuple-element.29), channel_id=1, source_target_pairs={{0,1},{2,3},{4,5},{6,7},{8,9},{10,11},{12,13},{14,15},{1,0},{3,2},... | collective-permute-start | bytes 73736 | tf_op jit(solution)/shard_map/ppermute | solution.py:442
  33.9 9.7 %conv.1.inner_ref = f32[3072,128]{1,0:T(8,128)S(1)} custom-call(s32[8,16]{1,0:T(8,128)S(1)} %copy-done.8, s32[8,16]{1,0:T(8,128)S(1)} %copy-done.9, s32[8,16]{1,0:T(8,128)S(1)} %copy-done.10, f32[8,16]{1,0:T(8,128)S(1)} %copy-done.11, f32[3072,128]{1,0:T(8,128)S(1)} %bitcast.15, bf16[768,128]{1,0:T(8,128)(2,1)S(1)} %collective-permute-done.up_ref, ...), custom_call_target="tpu_custom_call" | custom-call | tf_op jit(solution)/shard_map/conv/pallas_call | solution.py:454
  43.6 0.0 copy-start.3
  43.6 0.0 copy-start.6
  43.7 0.0 collective-permute-done.2.far_ref
  43.7 0.0 collective-permute-done.3.near_ref
  43.7 2.9 %seam.1 = (f32[3072,128]{1,0:T(8,128)S(1)}, bf16[3072,128]{1,0:T(8,128)(2,1)S(1)}) custom-call(s32[1]{0:T(128)} %bitcast.core_ref, s32[8,16]{1,0:T(8,128)S(1)} %copy-done.8, s32[8,16]{1,0:T(8,128)S(1)} %copy-done.9, s32[8,16]{1,0:T(8,128)S(1)} %copy-done.10, f32[8,16]{1,0:T(8,128)S(1)} %copy-done.11, f32[3072,128]{1,0:T(8,128)S(1)} %conv.1.inner_ref, ...), custom_call_target="tpu_custom_call" | custom-call | tf_op jit(solution)/shard_map/seam/pallas_call | solution.py:461
  46.6 21.4 %all_to_all.20.recv_ref = bf16[32,96,128]{2,1,0:T(8,128)(2,1)S(1)} all-to-all(bf16[32,96,128]{2,1,0:T(8,128)(2,1)S(1)} %bitcast.21), channel_id=1, replica_groups=mesh['zl'=8,'y'=4,'zh'=2,'x'=4,'core'=2] {'x','y','core'}, dimensions={0} | all-to-all | bytes 1572864 | tf_op jit(solution)/shard_map/all_to_all | solution.py:398
  68.0 1.7 %fourier.1 = bf16[512,384]{1,0:T(8,128)(2,1)} custom-call(bf16[32,96,128]{2,1,0:T(8,128)(2,1)S(1)} %all_to_all.20.recv_ref, bf16[512,1024]{1,0:T(8,128)(2,1)S(1)} %copy-done.6, bf16[384,384]{1,0:T(8,128)(2,1)S(1)} %copy-done.3), custom_call_target="tpu_custom_call" | custom-call | tf_op jit(solution)/shard_map/fourier/pallas_call | solution.py:470
  69.7 4.4 %all-to-all-start.1 = ((bf16[16,32,384]{2,1,0:T(8,128)(2,1)}), bf16[16,32,384]{2,1,0:T(8,128)(2,1)S(1)}, u32[]{:S(2)}, u32[]{:S(2)}) async-start(bf16[16,32,384]{2,1,0:T(8,128)(2,1)} %bitcast.5), calls=%async_computation.1 | async-start | bytes 786432 | tf_op jit(solution)/shard_map/all_to_all | solution.py:398
  74.1 7.6 %legendre.1.table_ref = bf16[2,16,256,256]{3,2,1,0:T(8,128)(2,1)} custom-call(s32[1]{0:T(128)} %bitcast.7.place_ref, f32[2,256]{1,0:T(2,128)} %constant.44.clone.degree_ref, f32[256,128]{1,0:T(8,128)} %constant.45.clone.term_ref, f32[8,256]{1,0:T(8,128)} %constant.46.clone.lat_ref), custom_call_target="tpu_custom_call" | custom-call | tf_op jit(solution)/shard_map/legendre/pallas_call | solution.py:445
  81.7 11.8 %all-to-all-done.1 = bf16[16,32,384]{2,1,0:T(8,128)(2,1)S(1)} async-done(((bf16[16,32,384]{2,1,0:T(8,128)(2,1)}), bf16[16,32,384]{2,1,0:T(8,128)(2,1)S(1)}, u32[]{:S(2)}, u32[]{:S(2)}) %all-to-all-start.1) | async-done | bytes 393248 | tf_op jit(solution)/shard_map/all_to_all | solution.py:398
  93.5 6.0 %spectral.1 = bf16[512,384]{1,0:T(8,128)(2,1)S(1)} custom-call(bf16[512,384]{1,0:T(8,128)(2,1)S(1)} %bitcast.17, bf16[2,16,256,256]{3,2,1,0:T(8,128)(2,1)} %legendre.1.table_ref, f32[256,128]{1,0:T(8,128)S(1)} %maximum_bitcast_fusion.filter_ref), custom_call_target="tpu_custom_call" | custom-call | tf_op jit(solution)/shard_map/spectral/pallas_call | solution.py:474
  99.6 28.0 %all_to_all.21 = bf16[16,32,384]{2,1,0:T(8,128)(2,1)S(1)} all-to-all(bf16[16,32,384]{2,1,0:T(8,128)(2,1)S(1)} %bitcast.18), channel_id=1, replica_groups=mesh['zl'=8,'y'=4,'zh'=2,'x'=4,'core'=2] {'zh','zl'}, dimensions={0} | all-to-all | bytes 786432 | tf_op jit(solution)/shard_map/all_to_all | solution.py:398
  127.6 1.4 inverse.1
  129.0 24.8 %all_to_all.22 = bf16[32,96,128]{2,1,0:T(8,128)(2,1)S(1)} all-to-all(bf16[32,96,128]{2,1,0:T(8,128)(2,1)S(1)} %inverse.1), channel_id=1, replica_groups=mesh['zl'=8,'y'=4,'zh'=2,'x'=4,'core'=2] {'x','y','core'}, dimensions={0} | all-to-all | bytes 1572864 | tf_op jit(solution)/shard_map/all_to_all | solution.py:398
  153.7 2.2 %mix.1 = f32[3072,128]{1,0:T(8,128)} custom-call(bf16[3072,128]{1,0:T(8,128)(2,1)S(1)} %bitcast.16, f32[3072,128]{1,0:T(8,128)S(1)} %get-tuple-element.33.after_ref, bf16[384,384]{1,0:T(8,128)(2,1)S(1)} %get-tuple-element.34.mixt_ref), custom_call_target="tpu_custom_call" | custom-call | tf_op jit(solution)/shard_map/mix/pallas_call | solution.py:492
  (23 shorter events, 0.1 us)
Async XLA Ops:
  0.0 7.1 %copy-start = (f32[384,256]{1,0:T(8,128)S(1)}, f32[384,256]{1,0:T(8,128)}, u32[]{:S(2)}) copy-start(f32[384,256]{1,0:T(8,128)} %param.22) | copy-start | bytes 1179652
  0.0 1.5 copy-start.1
  1.5 5.7 %copy-start.12 = (f32[384]{0:T(512)S(1)}, f32[384]{0:T(512)}, u32[]{:S(2)}) copy-start(f32[384]{0:T(512)} %param.21) | copy-start | bytes 4612
  1.5 10.8 %copy-start.2 = (f32[384,8,128]{2,1,0:T(8,128)S(1)}, f32[384,8,128]{2,1,0:T(8,128)}, u32[]{:S(2)}) copy-start(f32[384,8,128]{2,1,0:T(8,128)} %param.15) | copy-start | bytes 4718596
  1.6 8.6 %collective-permute-start = (bf16[768,128]{1,0:T(8,128)(2,1)S(1)}, bf16[768,128]{1,0:T(8,128)(2,1)S(1)}, u32[]{:S(2)}, u32[]{:S(2)}) collective-permute-start(bf16[768,128]{1,0:T(8,128)(2,1)S(1)} %get-tuple-element.20), channel_id=1, source_target_pairs={{0,16},{16,32},{32,48},{48,64},{64,80},{80,96},{96,112},{112,128},... | collective-permute-start | bytes 589832 | tf_op jit(solution)/shard_map/ppermute | solution.py:426
  5.8 6.4 %collective-permute-start.1 = (bf16[768,128]{1,0:T(8,128)(2,1)S(1)}, bf16[768,128]{1,0:T(8,128)(2,1)S(1)}, u32[]{:S(2)}, u32[]{:S(2)}) collective-permute-start(bf16[768,128]{1,0:T(8,128)(2,1)S(1)} %get-tuple-element.21), channel_id=1, source_target_pairs={{16,0},{32,16},{48,32},{64,48},{80,64},{96,80},{112,96},{128,112},... | collective-permute-start | bytes 589832 | tf_op jit(solution)/shard_map/ppermute | solution.py:427
  7.4 1.3 copy-start.4
  8.6 1.0 copy-start.7
  9.6 24.2 %copy-start.8 = (s32[8,16]{1,0:T(8,128)S(1)}, s32[8,16]{1,0:T(8,128)}, u32[]{:S(2)}) copy-start(s32[8,16]{1,0:T(8,128)} %dlat_ref.3) | copy-start | bytes 1540
  9.6 24.3 %copy-start.9 = (s32[8,16]{1,0:T(8,128)S(1)}, s32[8,16]{1,0:T(8,128)}, u32[]{:S(2)}) copy-start(s32[8,16]{1,0:T(8,128)} %dlon_ref.3) | copy-start | bytes 1540
  9.6 24.3 %copy-start.10 = (s32[8,16]{1,0:T(8,128)S(1)}, s32[8,16]{1,0:T(8,128)}, u32[]{:S(2)}) copy-start(s32[8,16]{1,0:T(8,128)} %basis_ref.3) | copy-start | bytes 1540
  9.6 24.3 %copy-start.11 = (f32[8,16]{1,0:T(8,128)S(1)}, f32[8,16]{1,0:T(8,128)}, u32[]{:S(2)}) copy-start(f32[8,16]{1,0:T(8,128)} %quad_ref.3) | copy-start | bytes 1540
  12.9 30.8 %collective-permute-start.2 = (bf16[32,384]{1,0:T(8,128)(2,1)S(1)}, bf16[32,384]{1,0:T(8,128)(2,1)S(1)}, u32[]{:S(2)}, u32[]{:S(2)}) collective-permute-start(bf16[32,384]{1,0:T(8,128)(2,1)S(1)} %get-tuple-element.28), channel_id=1, source_target_pairs={{1,2},{3,4},{5,6},{7,8},{9,10},{11,12},{13,14},{15,0},{2,1},{4,3},... | collective-permute-start | bytes 73736 | tf_op jit(solution)/shard_map/ppermute | solution.py:441
  18.7 25.0 %collective-permute-start.3 = (bf16[32,384]{1,0:T(8,128)(2,1)S(1)}, bf16[32,384]{1,0:T(8,128)(2,1)S(1)}, u32[]{:S(2)}, u32[]{:S(2)}) collective-permute-start(bf16[32,384]{1,0:T(8,128)(2,1)S(1)} %get-tuple-element.29), channel_id=1, source_target_pairs={{0,1},{2,3},{4,5},{6,7},{8,9},{10,11},{12,13},{14,15},{1,0},{3,2},... | collective-permute-start | bytes 73736 | tf_op jit(solution)/shard_map/ppermute | solution.py:442
  43.6 24.4 %copy-start.3 = (bf16[384,384]{1,0:T(8,128)(2,1)S(1)}, bf16[384,384]{1,0:T(8,128)(2,1)}, u32[]{:S(2)}) copy-start(bf16[384,384]{1,0:T(8,128)(2,1)} %constant.48.clone.lane_ref) | copy-start | bytes 884740
  43.6 24.4 %copy-start.6 = (bf16[512,1024]{1,0:T(8,128)(2,1)S(1)}, bf16[512,1024]{1,0:T(8,128)(2,1)}, u32[]{:S(2)}) copy-start(bf16[512,1024]{1,0:T(8,128)(2,1)} %constant.47.clone.lon_ref) | copy-start | bytes 3145732
  69.7 23.8 %all-to-all-start.1 = ((bf16[16,32,384]{2,1,0:T(8,128)(2,1)}), bf16[16,32,384]{2,1,0:T(8,128)(2,1)S(1)}, u32[]{:S(2)}, u32[]{:S(2)}) async-start(bf16[16,32,384]{2,1,0:T(8,128)(2,1)} %bitcast.5), calls=%async_computation.1 | async-start | bytes 786432 | tf_op jit(solution)/shard_map/all_to_all | solution.py:398
  93.5 34.0 %copy-start.5 = (bf16[512,1024]{1,0:T(8,128)(2,1)S(1)}, bf16[512,1024]{1,0:T(8,128)(2,1)}, u32[]{:S(2)}) copy-start(bf16[512,1024]{1,0:T(8,128)(2,1)} %constant.49.clone.lon_ref) | copy-start | bytes 3145732
